TPU v7x, 512 devices: a whole 4x4x16 slice. The times are simulated.
512 devices in a mesh: mem: 128 (over x, z, core), grp: 4 (over y).
Axes of the slice: x: 4, y: 4, z: 16, core: 2. Of those that a mesh axis runs over, the one named last changes fastest.
Arguments:
- prior_members: bfloat16 [256, 512, 256], P('mem', 'grp'), may hold values from -6 to 6
- mapped_prior: bfloat16 [256, 512, 1024], P('mem', 'grp'), may hold values from -6 to 6
- departure: float32 [512, 1024], P(('grp', 'mem')), may hold values from -18 to 18
- precision_factor: float32 [512, 1024], P(('grp', 'mem')), may hold values from 0.02 to 0.5
- measured_lines: int32 [512], P(('grp', 'mem')), may hold values from 256 to 1024, as said below
Outputs:
- analysis: bfloat16 [256, 512, 256], P('mem', 'grp')
Inputs may be any that keep to these rules, and one draw needn't show every extreme that they name: Only the first measured_lines rows of a patch's observation block are used; some patch has exactly 1024 rows and some exactly 256.
All inputs are finite; a program needn't handle non-finite values.
Results may differ from a plain program's by a relative error of at most 0.008.
Values may be sent and summed in bfloat16 or wider, within the bound.
A program may use at most 64 MiB of HBM per device.

v0:
```python
import math

import jax
import jax.numpy as jnp
from jax import lax
from jax.sharding import Mesh
from jax.sharding import PartitionSpec as P

OBS_BLK = 128
ITERS = 5
MEM = ("mem_0", "mem_1", "mem_2")
GRP_MEM = ("grp", "mem_0", "mem_1", "mem_2")


highest = lax.Precision.HIGHEST


def side_by_side(arrays, axis, split_dim, concat_dim, along):
    both = jnp.concatenate(arrays, axis=along)
    result, at, finished = (
        lax.all_to_all(both, axis, split_axis=split_dim, concat_axis=concat_dim, tiled=True),
        0,
        [],
    )
    for a in arrays:
        finished.append(lax.slice_in_dim(result, at, at + a.shape[along], axis=along))
        at += a.shape[along]
    return tuple(finished)


def in_blocks(array, dim, size):
    before, after = (array.shape[:dim], array.shape[dim + 1 :])
    return jnp.moveaxis(array.reshape(*before, size, -1, *after), dim, 0)


def joined_along(tiles, dim):
    tiles = jnp.moveaxis(tiles, 0, dim)
    shape = tiles.shape
    return tiles.reshape(*shape[:dim], shape[dim] * shape[dim + 1], *shape[dim + 2 :])


def exchange_in_order(tiles, axes, order):
    shape = [lax.axis_size(a) for a in axes]
    tiles = tiles.reshape(*shape, *tiles.shape[1:])
    for k in order:
        tiles = lax.all_to_all(tiles, axes[k], split_axis=k, concat_axis=k, tiled=True)
    return tiles.reshape(-1, *tiles.shape[len(axes) :])


def core_and_chips(array, groups, order, split_dim, concat_dim):
    size = lax.axis_size(groups[0]) * lax.axis_size(groups[1])
    tiles = in_blocks(array, split_dim, size)
    return joined_along(exchange_in_order(tiles, groups, order), concat_dim)


def block_terms(totals, obs_piece, weight_blk, innov_blk, first_row, lines_in_play):
    gram_total, pull_vec = totals
    values = obs_piece.astype(jnp.float32)
    deviat = values - jnp.mean(values, axis=0, keepdims=True)
    row_ids = first_row + jnp.arange(obs_piece.shape[1], dtype=jnp.int32)
    weights = jnp.where(row_ids < lines_in_play, weight_blk, jnp.float32(0.0))
    weighted = deviat * weights[None, :]
    gram_total = gram_total + jnp.dot(weighted, deviat.T, precision=highest)
    pull_vec = pull_vec + jnp.dot(weighted, innov_blk, precision=highest)
    return (gram_total, pull_vec)


def empty_terms(members):
    return (jnp.zeros((members, members), jnp.float32), jnp.zeros((members,), jnp.float32))


def own_terms(measurement_data, departure, precision_factor, measured_lines):
    members = measurement_data.shape[0]

    def patch_terms(domain_number):
        lines_in_play = measured_lines[domain_number]
        column = lax.dynamic_index_in_dim(measurement_data, domain_number, 1, keepdims=False)
        departure_line = lax.dynamic_index_in_dim(departure, domain_number, 0, keepdims=False)
        line_precision_list = lax.dynamic_index_in_dim(
            precision_factor, domain_number, 0, keepdims=False
        )
        blocks_due = (lines_in_play + OBS_BLK - 1) // OBS_BLK

        def block_step(block_no, totals):
            first_row = block_no * OBS_BLK
            obs_piece = lax.dynamic_slice_in_dim(column, first_row, OBS_BLK, 1)
            weight_blk = lax.dynamic_slice_in_dim(line_precision_list, first_row, OBS_BLK, 0)
            innov_blk = lax.dynamic_slice_in_dim(departure_line, first_row, OBS_BLK, 0)
            return block_terms(totals, obs_piece, weight_blk, innov_blk, first_row, lines_in_play)

        return lax.fori_loop(0, blocks_due, block_step, empty_terms(members))

    return lax.map(patch_terms, jnp.arange(measurement_data.shape[1], dtype=jnp.int32))


def finish(gram_total, pull_vec, patch_state):
    members = gram_total.shape[1]
    identity = jnp.eye(members, dtype=jnp.float32)
    system = gram_total + jnp.float32(members - 1) * identity[None]
    fro_scale = jnp.sqrt(jnp.sum(system * system, axis=(1, 2)))
    iterate = system / fro_scale[:, None, None]
    inv_root = jnp.broadcast_to(identity, system.shape)
    for sweep in range(ITERS):
        factor = 0.5 * (
            3.0 * identity[None] - jnp.einsum("pij,pjk->pik", inv_root, iterate, precision=highest)
        )
        iterate = jnp.einsum("pij,pjk->pik", iterate, factor, precision=highest)
        inv_root = jnp.einsum("pij,pjk->pik", factor, inv_root, precision=highest)
    inner = jnp.einsum("pij,pj->pi", inv_root, pull_vec, precision=highest)
    mean_shift = jnp.einsum("pij,pj->pi", inv_root, inner, precision=highest) / fro_scale[:, None]
    transform = (math.sqrt(members - 1) / jnp.sqrt(fro_scale))[
        :, None, None
    ] * inv_root + mean_shift[:, :, None]
    grid_quantities = patch_state.astype(jnp.float32)
    center = jnp.mean(grid_quantities, axis=0, keepdims=True)
    spread = grid_quantities - center
    result = center + jnp.einsum("kpv,pkl->lpv", spread, transform, precision=highest)
    return result.astype(jnp.bfloat16)


def local(prior_members, mapped_prior, departure, precision_factor, measured_lines):
    patch_state, measurement_data = side_by_side((prior_members, mapped_prior), MEM, 1, 0, 2)
    gram_total, pull_vec = own_terms(measurement_data, departure, precision_factor, measured_lines)
    analysed = finish(gram_total, pull_vec, patch_state)
    return core_and_chips(analysed, (("mem_0", "mem_1"), "mem_2"), (1, 0), 0, 1)


def solution(mesh):
    split = Mesh(
        mesh.devices.reshape(4, 16, 2, mesh.shape["grp"]), ("mem_0", "mem_1", "mem_2", "grp")
    )
    return jax.shard_map(
        local,
        mesh=split,
        in_specs=(
            P(MEM, "grp", None),
            P(MEM, "grp", None),
            P(GRP_MEM, None),
            P(GRP_MEM, None),
            P(GRP_MEM),
        ),
        out_specs=P(MEM, "grp", None),
        check_vma=False,
    )
```

profile of v0, /device:TPU:1, one launch (start us, length us, event | category | flops | bytes accessed | tf_op | source)
XLA Modules:
  0.0 118.2 jit_solution(6720132693613255704)
XLA Ops:
  0.0 1.1 pad_maximum_fusion
  1.1 1.5 %copy.13 = bf16[2,128,1280]{2,0,1:T(2,128)(2,1)} copy(bf16[2,128,1280]{2,1,0:T(8,128)(2,1)S(1)} %pad_maximum_fusion) | data formatting | bytes 1310720 | tf_op jit(solution)/shard_map/concatenate | solution.py:19
  2.6 20.4 %all-to-all-start = ((bf16[2,128,1280]{2,0,1:T(2,128)(2,1)}), bf16[2,128,1280]{2,0,1:T(2,128)(2,1)S(1)}, u32[]{:S(2)}, u32[]{:S(2)}) async-start(bf16[2,128,1280]{2,0,1:T(2,128)(2,1)} %copy.13), calls=%async_computation | async-start | bytes 1310720 | tf_op jit(solution)/shard_map/all_to_all | solution.py:21
  23.7 37.5 %all-to-all-done = bf16[2,128,1280]{2,0,1:T(2,128)(2,1)S(1)} async-done(((bf16[2,128,1280]{2,0,1:T(2,128)(2,1)}), bf16[2,128,1280]{2,0,1:T(2,128)(2,1)S(1)}, u32[]{:S(2)}, u32[]{:S(2)}) %all-to-all-start) | async-done | bytes 655392 | tf_op jit(solution)/shard_map/all_to_all | solution.py:21
  61.6 8.8 %while.21 = (s32[]{:T(128)}, f32[256,256]{1,0:T(8,128)S(1)}, f32[256]{0:T(256)S(1)}, s32[]{:T(128)}, bf16[256,1024]{1,0:T(8,128)(2,1)S(1)}, /*index=5*/s32[]{:T(...) while((s32[]{:T(128)}, f32[256,256]{1,0:T(8,128)S(1)}, ...), condition=%wide.region_3.4_spmd, body=%wide.region_1.3_spmd.sunk | while | flops 101450376 | bytes 798387 | solution.py:91
  61.6 1.4 %compare_select_fusion.2 = (f32[128]{0:T(128)S(1)}, f32[128]{0:T(128)S(1)}) fusion(f32[1024]{0:T(1024)} %get-tuple-element.176, s32[]{:T(128)S(6)} %select_n.27, s32[]{:T(128)} %get-tuple-element.175, s32[]{:T(128)S(6)} %mul.129, f32[128]{0:T(128)S(1)} %convert_reduce_fusion.3), kind=kLoop, calls=%fused_computation.12.clone.1 | loop fusion | flops 512 | bytes 2060 | tf_op jit(solution)/shard_map/while/body/eval_jaxpr/while/body/jit(_where)/select_n | solution.py:61
  63.0 0.5 convolution_add_fusion.3
  63.5 0.9 fusion.79
  64.6 1.4 %compare_select_fusion.2 = (f32[128]{0:T(128)S(1)}, f32[128]{0:T(128)S(1)}) fusion(f32[1024]{0:T(1024)} %get-tuple-element.176, s32[]{:T(128)S(6)} %select_n.27, s32[]{:T(128)} %get-tuple-element.175, s32[]{:T(128)S(6)} %mul.129, f32[128]{0:T(128)S(1)} %convert_reduce_fusion.3), kind=kLoop, calls=%fused_computation.12.clone.1 | loop fusion | flops 512 | bytes 2060 | tf_op jit(solution)/shard_map/while/body/eval_jaxpr/while/body/jit(_where)/select_n | solution.py:61
  66.0 0.5 convolution_add_fusion.3
  66.4 0.9 fusion.79
  67.5 1.4 %compare_select_fusion.2 = (f32[128]{0:T(128)S(1)}, f32[128]{0:T(128)S(1)}) fusion(f32[1024]{0:T(1024)} %get-tuple-element.176, s32[]{:T(128)S(6)} %select_n.27, s32[]{:T(128)} %get-tuple-element.175, s32[]{:T(128)S(6)} %mul.129, f32[128]{0:T(128)S(1)} %convert_reduce_fusion.3), kind=kLoop, calls=%fused_computation.12.clone.1 | loop fusion | flops 512 | bytes 2060 | tf_op jit(solution)/shard_map/while/body/eval_jaxpr/while/body/jit(_where)/select_n | solution.py:61
  68.9 0.5 convolution_add_fusion.3
  69.3 0.9 fusion.79
  70.3 0.7 multiply_reduce_fusion
  71.7 0.3 fusion.17
  72.0 0.4 fusion.29
  72.7 0.4 fusion.16
  73.1 0.4 fusion.37
  73.5 0.4 fusion.36
  73.9 0.4 fusion.15
  74.3 0.4 fusion.39
  74.6 0.4 fusion.38
  75.0 0.4 fusion.14
  75.4 0.4 fusion.41
  75.8 0.4 fusion.40
  76.3 0.4 fusion.13
  76.7 0.4 fusion.42
  77.7 0.7 fusion.18
  78.6 5.0 %all_to_all.28 = bf16[64,2,2,1,256]{4,2,0,3,1:T(2,128)(2,1)S(1)} all-to-all(bf16[64,2,2,1,256]{4,2,0,3,1:T(2,128)(2,1)S(1)} %copy.14), channel_id=1, replica_groups=mesh['mem_0'=4,'mem_1'=16,'mem_2'=2,'grp'=4] {'mem_2'}, dimensions={1} | all-to-all | bytes 262144 | tf_op jit(solution)/shard_map/all_to_all | solution.py:46
  83.6 33.9 %all_to_all.29 = bf16[64,2,2,1,256]{4,2,1,3,0:T(2,128)(2,1)S(1)} all-to-all(bf16[64,2,2,1,256]{4,2,1,3,0:T(2,128)(2,1)S(1)} %copy.15), channel_id=1, replica_groups=mesh['mem_0'=4,'mem_1'=16,'mem_2'=2,'grp'=4] {'mem_0','mem_1'}, dimensions={0} | all-to-all | bytes 262144 | tf_op jit(solution)/shard_map/all_to_all | solution.py:46
  117.6 0.7 copy.18
  (18 shorter events, 1.8 us)
Async XLA Ops:
  2.6 58.6 %all-to-all-start = ((bf16[2,128,1280]{2,0,1:T(2,128)(2,1)}), bf16[2,128,1280]{2,0,1:T(2,128)(2,1)S(1)}, u32[]{:S(2)}, u32[]{:S(2)}) async-start(bf16[2,128,1280]{2,0,1:T(2,128)(2,1)} %copy.13), calls=%async_computation | async-start | bytes 1310720 | tf_op jit(solution)/shard_map/all_to_all | solution.py:21
where the time goes:
time: 120 us; the launch traced here: 118 us
  blocking collectives  38.9 us (32%)
  waiting for transfers between devices  37.5 us (31%)
  starting transfers between devices  20.4 us (17%)
  matrix products  10.5 us (9%)
  other arithmetic  6.38 us (5%)
  local copies, waits for them, and re-layouts  2.74 us (2%)
  between operations  1.65 us (1%)
    all_to_all x2, blocking collectives, exchange_in_order(): lax.all_to_all(tiles, axes[k], split_axis=k, concat_axis=k, tiled=True)  38.9 us
    all_to_all x1, waiting for transfers between devices, side_by_side(): lax.all_to_all(both, axis, split_axis=split_dim, concat_axis=concat_dim,...  37.5 us
    all_to_all x1, starting transfers between devices, side_by_side(): lax.all_to_all(both, axis, split_axis=split_dim, concat_axis=concat_dim,...  20.4 us
    select_n x3, other arithmetic, block_terms(): weights = jnp.where(row_ids < lines_in_play, weight_blk, jnp.float32(0.0))  4.22 us
    dot_general x3, matrix products, block_terms(): pull_vec = pull_vec + jnp.dot(weighted, innov_blk, precision=highest)  2.71 us
  transfers between devices with their start and end apart: 1, of which 1 were waited for; matrix products, arithmetic and copies ran while one was open for 0% of the time, Pallas kernels for 0%

commit v1 on v0

v1 whole, which is shorter than its diff:
```python
import functools
import math

import jax
import jax.numpy as jnp
from jax import lax
from jax.experimental import pallas as pl
from jax.experimental.pallas import tpu as pltpu
from jax.sharding import Mesh
from jax.sharding import PartitionSpec as P

ITERS = 5
OWN = 2
CHUNK = 256
MEM = ("x", "z", "c")
GRP_MEM = ("grp", "x", "z", "c")
MESH_ID = pl.DeviceIdType.MESH

highest = lax.Precision.HIGHEST
f32 = jnp.float32
bf16 = jnp.bfloat16


def one_hot(rows, source_of):
    out_row = lax.broadcasted_iota(jnp.int32, (rows, rows), 0)
    in_row = lax.broadcasted_iota(jnp.int32, (rows, rows), 1)
    return jnp.where(in_row == source_of(out_row), f32(1.0), f32(0.0)).astype(bf16)


def moved(perm, rows):
    return jnp.dot(perm, rows, preferred_element_type=f32).astype(bf16)


def kernel(
    nx, nz, nc,
    prior_hbm, mapped_hbm, dep_ref, prec_ref, lines_ref, out_ref,
    raw, split_a, split_z, back_z, back_a, s1, ar, s2, zr, s3, zb, s4, ab, gram, pull, root, itr,
    raw_sem, a_send, a_recv, z_send, z_recv, zb_send, zb_recv, ab_send, ab_recv,
):
    na = nx * nc
    members = OWN * na * nz
    obs_chunks = mapped_hbm.shape[2] // CHUNK
    chunks = obs_chunks + 1
    patches = nx * nz * nc
    x, z, c = lax.axis_index("x"), lax.axis_index("z"), lax.axis_index("c")
    a = x * nc + c

    def raw_copies(k):
        if k < obs_chunks:
            src = lambda m: mapped_hbm.at[m, :, pl.ds(k * CHUNK, CHUNK)]
        else:
            src = lambda m: prior_hbm.at[m]
        return [
            pltpu.make_async_copy(src(m), raw.at[k, pl.ds(m * patches, patches)], raw_sem.at[k, m])
            for m in range(OWN)
        ]

    for k in range(chunks):
        for copy in raw_copies(k):
            copy.start()

    barrier = pltpu.get_barrier_semaphore()

    def greet_z(j, _):
        pl.semaphore_signal(
            barrier, inc=1, device_id={"z": lax.rem(z + j, nz)}, device_id_type=MESH_ID
        )
        return 0

    def greet_a(j, _):
        t = lax.rem(a + j, na)
        pl.semaphore_signal(
            barrier, inc=1, device_id={"x": t // nc, "c": lax.rem(t, nc)}, device_id_type=MESH_ID
        )
        return 0

    lax.fori_loop(1, nz, greet_z, 0)
    lax.fori_loop(1, na, greet_a, 0)

    split_a[...] = one_hot(
        members,
        lambda r: (r % OWN) * patches
        + (r // (OWN * nz * nc)) * (nz * nc)
        + ((r // OWN) % nz) * nc
        + (r // (OWN * nz)) % nc,
    )
    split_z[...] = one_hot(
        members, lambda r: ((r // OWN) % na) * (OWN * nz) + (r // (OWN * na)) * OWN + r % OWN
    )
    back_z[...] = one_hot(
        members, lambda r: ((r // OWN) % nz) * (OWN * na) + (r // (OWN * nz)) * OWN + r % OWN
    )
    back_a[...] = one_hot(
        members,
        lambda r: ((r // (nz * nc)) % nx) * (OWN * nz * nc)
        + (r % nc) * (OWN * nz)
        + ((r // nc) % nz) * OWN
        + r // patches,
    )

    def a_copy(src, dst, send, recv, j):
        t = lax.rem(a + j, na)
        return pltpu.make_async_remote_copy(
            src_ref=src.at[t], dst_ref=dst.at[a], send_sem=send, recv_sem=recv,
            device_id={"x": t // nc, "c": lax.rem(t, nc)}, device_id_type=MESH_ID,
        )

    def z_copy(src, dst, send, recv, j):
        step = ((j + 1) // 2) * (1 - 2 * (j % 2))
        t = lax.rem(z + nz // 2 + step, nz)
        return pltpu.make_async_remote_copy(
            src_ref=src.at[t], dst_ref=dst.at[z], send_sem=send, recv_sem=recv,
            device_id={"z": t}, device_id_type=MESH_ID,
        )

    def all_a(src, dst, send, recv):
        def body(j, _):
            a_copy(src, dst, send, recv, j).start()
            return 0

        lax.fori_loop(1, na, body, 0)

    def all_z(src, dst, send, recv):
        def body(j, _):
            z_copy(src, dst, send, recv, j).start()
            return 0

        lax.fori_loop(0, nz - 1, body, 0)

    def arrived(ref, sem, n):
        part = ref.at[pl.ds(0, n)]
        pltpu.make_async_copy(part, part, sem).wait()

    def stage_one(k):
        for copy in raw_copies(k):
            copy.wait()
        s1[k] = moved(split_a[...], raw[k]).reshape(s1.shape[1:])
        ar[k, a] = s1[k, a]

    stage_one(0)
    pl.semaphore_wait(barrier, (nz - 1) + (na - 1))
    all_a(s1.at[0], ar.at[0], a_send.at[0], a_recv.at[0])
    for k in range(1, chunks):
        stage_one(k)
        all_a(s1.at[k], ar.at[k], a_send.at[k], a_recv.at[k])

    for k in range(chunks):
        arrived(ar.at[k], a_recv.at[k], na - 1)
        s2[k] = moved(split_z[...], ar[k].reshape(members, CHUNK)).reshape(s2.shape[1:])
        all_z(s2.at[k], zr.at[k], z_send.at[k], z_recv.at[k])
        zr[k, z] = s2[k, z]

    lines = lines_ref[0]
    eye = (
        lax.broadcasted_iota(jnp.int32, (members, members), 0)
        == lax.broadcasted_iota(jnp.int32, (members, members), 1)
    )
    identity = jnp.where(eye, f32(1.0), f32(0.0))
    gram[...] = f32(members - 1) * identity
    pull[...] = jnp.zeros_like(pull)
    for k in range(obs_chunks):
        arrived(zr.at[k], z_recv.at[k], nz - 1)
        values = zr[k].reshape(members, CHUNK).astype(f32)
        deviat = values - jnp.mean(values, axis=0, keepdims=True)
        row_ids = k * CHUNK + lax.broadcasted_iota(jnp.int32, (1, CHUNK), 1)
        cols = pl.ds(k * CHUNK, CHUNK)
        weights = jnp.where(row_ids < lines, prec_ref[:, cols], f32(0.0))
        weighted = deviat * weights
        gram[...] += lax.dot_general(
            weighted, deviat, (((1,), (1,)), ((), ())), precision=highest,
            preferred_element_type=f32,
        )
        pull[...] += jnp.sum(weighted * dep_ref[:, cols], axis=1, keepdims=True)

    def dot(p, q):
        return jnp.dot(p, q, precision=highest, preferred_element_type=f32)

    system = gram[...]
    scale = jnp.sqrt(jnp.sum(jnp.sum(system * system, axis=1, keepdims=True), axis=0, keepdims=True))
    itr[...] = system / scale
    root[...] = identity
    for sweep in range(ITERS):
        if sweep == 0:
            factor = 1.5 * identity - 0.5 * itr[...]
            root[...] = factor
        else:
            factor = 1.5 * identity - 0.5 * dot(root[...], itr[...])
            root[...] = dot(factor, root[...])
        if sweep < ITERS - 1:
            itr[...] = dot(itr[...], factor)

    inv_root = root[...]
    inner = jnp.sum(inv_root * pull[...], axis=0, keepdims=True)
    shift = jnp.sum(inv_root * inner, axis=1, keepdims=True) / scale
    shift = jnp.sum(jnp.where(eye, shift, f32(0.0)), axis=0, keepdims=True)
    transform = (math.sqrt(members - 1) / jnp.sqrt(scale)) * inv_root + shift

    arrived(zr.at[obs_chunks], z_recv.at[obs_chunks], nz - 1)
    quantities = zr[obs_chunks].reshape(members, CHUNK).astype(f32)
    center = jnp.mean(quantities, axis=0, keepdims=True)
    result = center + dot(transform, quantities - center)
    s3[...] = result.astype(bf16).reshape(s3.shape)
    all_z(s3, zb, zb_send, zb_recv)
    zb[z] = s3[z]
    arrived(zb, zb_recv, nz - 1)
    s4[...] = moved(back_z[...], zb[...].reshape(members, CHUNK)).reshape(s4.shape)
    all_a(s4, ab, ab_send, ab_recv)
    ab[a] = s4[a]
    arrived(ab, ab_recv, na - 1)
    out_ref[...] = moved(back_a[...], ab[...].reshape(members, CHUNK)).reshape(out_ref.shape)

    for k in range(chunks):
        arrived(s1.at[k], a_send.at[k], na - 1)
        arrived(s2.at[k], z_send.at[k], nz - 1)
    arrived(s3, zb_send, nz - 1)
    arrived(s4, ab_send, na - 1)


def solution(mesh):
    nx, nz, nc = 4, 16, 2
    split = Mesh(mesh.devices.reshape(nx, nz, nc, mesh.shape["grp"]), ("x", "z", "c", "grp"))
    na = nx * nc
    members = OWN * na * nz

    def local(prior_members, mapped_prior, departure, precision_factor, measured_lines):
        chunks = mapped_prior.shape[2] // CHUNK + 1
        square = pltpu.VMEM((members, members), f32)
        perm = pltpu.VMEM((members, members), bf16)
        by_a = (na, OWN * nz, CHUNK)
        by_z = (nz, OWN * na, CHUNK)
        dma = pltpu.SemaphoreType.DMA
        return pl.pallas_call(
            functools.partial(kernel, nx, nz, nc),
            out_shape=jax.ShapeDtypeStruct(prior_members.shape, bf16),
            in_specs=[
                pl.BlockSpec(memory_space=pl.ANY),
                pl.BlockSpec(memory_space=pl.ANY),
                pl.BlockSpec(memory_space=pltpu.VMEM),
                pl.BlockSpec(memory_space=pltpu.VMEM),
                pl.BlockSpec(memory_space=pltpu.SMEM),
            ],
            out_specs=pl.BlockSpec(memory_space=pltpu.VMEM),
            scratch_shapes=[
                pltpu.VMEM((chunks, members, CHUNK), bf16),
                perm, perm, perm, perm,
                pltpu.VMEM((chunks, *by_a), bf16),
                pltpu.VMEM((chunks, *by_a), bf16),
                pltpu.VMEM((chunks, *by_z), bf16),
                pltpu.VMEM((chunks, *by_z), bf16),
                pltpu.VMEM(by_z, bf16),
                pltpu.VMEM(by_z, bf16),
                pltpu.VMEM(by_a, bf16),
                pltpu.VMEM(by_a, bf16),
                square,
                pltpu.VMEM((members, 1), f32),
                square,
                square,
                dma((chunks, OWN)),
                dma((chunks,)), dma((chunks,)),
                dma((chunks,)), dma((chunks,)),
                dma, dma, dma, dma,
            ],
            compiler_params=pltpu.CompilerParams(
                collective_id=0, has_side_effects=True, vmem_limit_bytes=48 << 20
            ),
        )(prior_members, mapped_prior, departure, precision_factor, measured_lines)

    return jax.shard_map(
        local,
        mesh=split,
        in_specs=(
            P(MEM, "grp", None),
            P(MEM, "grp", None),
            P(GRP_MEM, None),
            P(GRP_MEM, None),
            P(GRP_MEM),
        ),
        out_specs=P(MEM, "grp", None),
        check_vma=False,
    )
```

time: 120 us -> 71.3 us (0.59); the launches traced: 118 us -> 71 us
  Pallas kernels: 0 us -> 66.4 us
  blocking collectives: 38.9 us -> 0 us
  waiting for transfers between devices: 37.5 us -> 0 us
  starting transfers between devices: 20.4 us -> 0 us
  matrix products: 10.5 us -> 0 us
  other arithmetic: 6.38 us -> 0 us
  local copies, waits for them, and re-layouts: 2.74 us -> 3.97 us
    pallas_call x0 -> x1, Pallas kernels: none -> 66.4 us  [local(): pl.pallas_call(functools.partial(kernel, nx, nz, nc), out_shape=jax.Shape...]
    all_to_all x2 -> x0, blocking collectives: 38.9 us -> none  [exchange_in_order(): lax.all_to_all(tiles, axes[k], split_axis=k, concat_axis=k, tiled=True)]
    all_to_all x1 -> x0, waiting for transfers between devices: 37.5 us -> none  [side_by_side(): lax.all_to_all(both, axis, split_axis=split_dim, concat_axis=concat_dim,...]
    all_to_all x1 -> x0, starting transfers between devices: 20.4 us -> none  [side_by_side(): lax.all_to_all(both, axis, split_axis=split_dim, concat_axis=concat_dim,...]
    dot_general x23 -> x0, matrix products: 10.5 us -> none  [the longest x3 2.71 us: block_terms(): pull_vec = pull_vec + jnp.dot(weighted, innov_blk, precision=highest)]
    select_n x3 -> x0, other arithmetic: 4.22 us -> none  [block_terms(): weights = jnp.where(row_ids < lines_in_play, weight_blk, jnp.float32(0.0))]
    unnamed x0 -> x9, local copies, waits for them, and re-layouts: none -> 3.97 us
    concatenate x1 -> x0, local copies, waits for them, and re-layouts: 1.51 us -> none  [side_by_side(): both = jnp.concatenate(arrays, axis=along)]
  transfers between devices with their start and end apart: 1 -> 0, of which waited for: 1 -> 0; matrix products, arithmetic and copies ran while one was open for 0% -> 0% of each run, Pallas kernels for 0% -> 0%
where the time goes in v1:
time: 71.3 us; the launch traced here: 71 us
  Pallas kernels  66.4 us (93%)
  local copies, waits for them, and re-layouts  3.97 us (6%)
    pallas_call x1, Pallas kernels, local(): pl.pallas_call(functools.partial(kernel, nx, nz, nc), out_shape=jax.Shape...  66.4 us
    unnamed x9, local copies, waits for them, and re-layouts  3.97 us

profile of v1, /device:TPU:1, one launch (start us, length us, event | category | flops | bytes accessed | tf_op | source)
XLA Modules:
  0.0 71.0 jit_solution(17534252449907644628)
XLA Ops:
  0.7 0.0 copy-start
  0.7 1.0 %copy-done = bf16[2,128,1024]{2,1,0:T(8,128)(2,1)S(1)} copy-done((bf16[2,128,1024]{2,1,0:T(8,128)(2,1)S(1)}, bf16[2,128,1024]{2,1,0:T(8,128)(2,1)}, u32[]{:S(2)}) %copy-start) | copy-done | bytes 524312
  1.7 0.0 copy-start.1
  1.7 0.9 %copy-done.1 = bf16[2,128,256]{2,1,0:T(8,128)(2,1)S(1)} copy-done((bf16[2,128,256]{2,1,0:T(8,128)(2,1)S(1)}, bf16[2,128,256]{2,1,0:T(8,128)(2,1)}, u32[]{:S(2)}) %copy-start.1) | copy-done | bytes 131096
  2.6 0.0 copy-start.2
  2.6 0.7 copy-done.2
  3.3 0.0 copy-start.3
  3.3 0.7 copy-done.3
  4.0 66.4 %shard_map.55 = bf16[2,128,256]{2,1,0:T(8,128)(2,1)S(1)} custom-call(bf16[2,128,256]{2,1,0:T(8,128)(2,1)S(1)} %copy-done.1, bf16[2,128,1024]{2,1,0:T(8,128)(2,1)S(1)} %copy-done, f32[1,1024]{1,0:T(1,128)S(1)} %copy-done.2, f32[1,1024]{1,0:T(1,128)S(1)} %copy-done.3, s32[1]{0:T(128)S(6)} %copy.7.lines_ref), custom_call_target="tpu_custom_call" | custom-call | tf_op jit(solution)/shard_map/pallas_call | solution.py:232
  70.4 0.7 copy.8
Async XLA Ops:
  0.7 1.0 %copy-start = (bf16[2,128,1024]{2,1,0:T(8,128)(2,1)S(1)}, bf16[2,128,1024]{2,1,0:T(8,128)(2,1)}, u32[]{:S(2)}) copy-start(bf16[2,128,1024]{2,1,0:T(8,128)(2,1)} %mapped_hbm.1) | copy-start | bytes 1572868
  1.7 0.9 %copy-start.1 = (bf16[2,128,256]{2,1,0:T(8,128)(2,1)S(1)}, bf16[2,128,256]{2,1,0:T(8,128)(2,1)}, u32[]{:S(2)}) copy-start(bf16[2,128,256]{2,1,0:T(8,128)(2,1)} %prior_hbm.1) | copy-start | bytes 393220
  2.6 0.7 copy-start.2
  3.3 0.7 copy-start.3

commit v2 on v1

--- a/solution.py
+++ b/solution.py
@@ -12,6 +12,7 @@
 ITERS = 5
 OWN = 2
 CHUNK = 256
+HALF = CHUNK // 2
 MEM = ("x", "z", "c")
 GRP_MEM = ("grp", "x", "z", "c")
 MESH_ID = pl.DeviceIdType.MESH
@@ -33,9 +34,9 @@
 
 def kernel(
     nx, nz, nc,
-    prior_hbm, mapped_hbm, dep_ref, prec_ref, lines_ref, out_ref,
-    raw, split_a, split_z, back_z, back_a, s1, ar, s2, zr, s3, zb, s4, ab, gram, pull, root, itr,
-    raw_sem, a_send, a_recv, z_send, z_recv, zb_send, zb_recv, ab_send, ab_recv,
+    prior_hbm, mapped_hbm, dep_hbm, prec_hbm, lines_ref, out_ref,
+    raw, dep_ref, prec_ref, split_a, split_z, back_z, back_a, nat_z, z_nat, s1, ar, s2, zr, s3, zb, s4, ab, gram, pull, root, itr,
+    raw_sem, row_sem, a_send, a_recv, z_send, z_recv, zb_send, zb_recv, ab_send, ab_recv,
 ):
     na = nx * nc
     members = OWN * na * nz
@@ -55,9 +56,15 @@
             for m in range(OWN)
         ]
 
+    row_copies = [
+        pltpu.make_async_copy(dep_hbm, dep_ref, row_sem.at[0]),
+        pltpu.make_async_copy(prec_hbm, prec_ref, row_sem.at[1]),
+    ]
     for k in range(chunks):
         for copy in raw_copies(k):
             copy.start()
+    for copy in row_copies:
+        copy.start()
 
     barrier = pltpu.get_barrier_semaphore()
 
@@ -77,26 +84,30 @@
     lax.fori_loop(1, nz, greet_z, 0)
     lax.fori_loop(1, na, greet_a, 0)
 
-    split_a[...] = one_hot(
-        members,
-        lambda r: (r % OWN) * patches
-        + (r // (OWN * nz * nc)) * (nz * nc)
-        + ((r // OWN) % nz) * nc
-        + (r // (OWN * nz)) % nc,
-    )
-    split_z[...] = one_hot(
-        members, lambda r: ((r // OWN) % na) * (OWN * nz) + (r // (OWN * na)) * OWN + r % OWN
-    )
-    back_z[...] = one_hot(
-        members, lambda r: ((r // OWN) % nz) * (OWN * na) + (r // (OWN * nz)) * OWN + r % OWN
-    )
-    back_a[...] = one_hot(
-        members,
-        lambda r: ((r // (nz * nc)) % nx) * (OWN * nz * nc)
-        + (r % nc) * (OWN * nz)
-        + ((r // nc) % nz) * OWN
-        + r // patches,
-    )
+    def natural(m, xi, zi, ci):
+        return m * patches + xi * (nz * nc) + zi * nc + ci
+
+    def of_natural(r):
+        return r // patches, (r // (nz * nc)) % nx, (r // nc) % nz, r % nc
+
+    def of_group(r):
+        return r % OWN, r // (OWN * nz * nc), (r // OWN) % nz, (r // (OWN * nz)) % nc
+
+    def of_ring(r):
+        return r % OWN, (r // (OWN * nc)) % nx, r // (OWN * na), (r // OWN) % nc
+
+    def group(m, xi, zi, ci):
+        return ((xi * nc + ci) * nz + zi) * OWN + m
+
+    def ring(m, xi, zi, ci):
+        return ((zi * nx + xi) * nc + ci) * OWN + m
+
+    nat_z[...] = one_hot(members, lambda r: natural(*of_ring(r)))
+    split_a[...] = one_hot(members, lambda r: natural(*of_group(r)))
+    split_z[...] = one_hot(members, lambda r: group(*of_ring(r)))
+    back_z[...] = one_hot(members, lambda r: ring(*of_group(r)))
+    back_a[...] = one_hot(members, lambda r: group(*of_natural(r)))
+    z_nat[...] = one_hot(members, lambda r: ring(*of_natural(r)))
 
     def a_copy(src, dst, send, recv, j):
         t = lax.rem(a + j, na)
@@ -127,29 +138,43 @@
 
         lax.fori_loop(0, nz - 1, body, 0)
 
-    def arrived(ref, sem, n):
+    def arrived(name, ref, sem, n):
         part = ref.at[pl.ds(0, n)]
-        pltpu.make_async_copy(part, part, sem).wait()
-
-    def stage_one(k):
+        with jax.named_scope(name):
+            pltpu.make_async_copy(part, part, sem).wait()
+
+    def by_group(perm, rows):
+        return moved(perm[...], rows).reshape(na, OWN * nz, -1)
+
+    def by_ring(perm, rows):
+        return moved(perm[...], rows).reshape(nz, OWN * na, -1)
+
+    for copy in raw_copies(0):
+        copy.wait()
+    s2[0] = by_ring(nat_z, raw[0])
+    zr[0, z] = s2[0, z]
+    with jax.named_scope("greet"):
+        pl.semaphore_wait(barrier, (nz - 1) + (na - 1))
+    all_z(s2.at[0], zr.at[0], z_send.at[0], z_recv.at[0])
+    for k in range(1, chunks):
         for copy in raw_copies(k):
             copy.wait()
-        s1[k] = moved(split_a[...], raw[k]).reshape(s1.shape[1:])
+        s1[k] = by_group(split_a, raw[k])
+        all_a(s1.at[k], ar.at[k], a_send.at[k], a_recv.at[k])
         ar[k, a] = s1[k, a]
-
-    stage_one(0)
-    pl.semaphore_wait(barrier, (nz - 1) + (na - 1))
-    all_a(s1.at[0], ar.at[0], a_send.at[0], a_recv.at[0])
     for k in range(1, chunks):
-        stage_one(k)
-        all_a(s1.at[k], ar.at[k], a_send.at[k], a_recv.at[k])
-
-    for k in range(chunks):
-        arrived(ar.at[k], a_recv.at[k], na - 1)
-        s2[k] = moved(split_z[...], ar[k].reshape(members, CHUNK)).reshape(s2.shape[1:])
+        arrived(f"a{k}", ar.at[k], a_recv.at[k], na - 1)
+        s2[k] = by_ring(split_z, ar[k].reshape(members, CHUNK))
         all_z(s2.at[k], zr.at[k], z_send.at[k], z_recv.at[k])
         zr[k, z] = s2[k, z]
 
+    arrived("z0", zr.at[0], z_recv.at[0], nz - 1)
+    s1[0] = by_group(back_z, zr[0].reshape(members, CHUNK))
+    all_a(s1.at[0], ar.at[0], a_send.at[0], a_recv.at[0])
+    ar[0, a] = s1[0, a]
+
+    for copy in row_copies:
+        copy.wait()
     lines = lines_ref[0]
     eye = (
         lax.broadcasted_iota(jnp.int32, (members, members), 0)
@@ -158,9 +183,15 @@
     identity = jnp.where(eye, f32(1.0), f32(0.0))
     gram[...] = f32(members - 1) * identity
     pull[...] = jnp.zeros_like(pull)
-    for k in range(obs_chunks):
-        arrived(zr.at[k], z_recv.at[k], nz - 1)
-        values = zr[k].reshape(members, CHUNK).astype(f32)
+    for k in (*range(1, obs_chunks - 1), 0, obs_chunks - 1):
+        if k == 0:
+            arrived("a0", ar.at[0], a_recv.at[0], na - 1)
+            values = jnp.dot(
+                split_z[...], ar[0].reshape(members, CHUNK), preferred_element_type=f32
+            )
+        else:
+            arrived(f"z{k}", zr.at[k], z_recv.at[k], nz - 1)
+            values = zr[k].reshape(members, CHUNK).astype(f32)
         deviat = values - jnp.mean(values, axis=0, keepdims=True)
         row_ids = k * CHUNK + lax.broadcasted_iota(jnp.int32, (1, CHUNK), 1)
         cols = pl.ds(k * CHUNK, CHUNK)
@@ -195,25 +226,44 @@
     shift = jnp.sum(jnp.where(eye, shift, f32(0.0)), axis=0, keepdims=True)
     transform = (math.sqrt(members - 1) / jnp.sqrt(scale)) * inv_root + shift
 
-    arrived(zr.at[obs_chunks], z_recv.at[obs_chunks], nz - 1)
+    arrived("zprior", zr.at[obs_chunks], z_recv.at[obs_chunks], nz - 1)
     quantities = zr[obs_chunks].reshape(members, CHUNK).astype(f32)
     center = jnp.mean(quantities, axis=0, keepdims=True)
-    result = center + dot(transform, quantities - center)
-    s3[...] = result.astype(bf16).reshape(s3.shape)
-    all_z(s3, zb, zb_send, zb_recv)
-    zb[z] = s3[z]
-    arrived(zb, zb_recv, nz - 1)
-    s4[...] = moved(back_z[...], zb[...].reshape(members, CHUNK)).reshape(s4.shape)
-    all_a(s4, ab, ab_send, ab_recv)
-    ab[a] = s4[a]
-    arrived(ab, ab_recv, na - 1)
-    out_ref[...] = moved(back_a[...], ab[...].reshape(members, CHUNK)).reshape(out_ref.shape)
+    spread = quantities - center
+
+    def result(half):
+        cols = slice(half * HALF, (half + 1) * HALF)
+        return (center[:, cols] + dot(transform, spread[:, cols])).astype(bf16)
+
+    s3[0] = result(0).reshape(nz, OWN * na, HALF)
+    all_z(s3.at[0], zb.at[0], zb_send.at[0], zb_recv.at[0])
+    zb[0, z] = s3[0, z]
+    s4[1] = by_group(back_z, result(1))
+    all_a(s4.at[1], ab.at[1], ab_send.at[1], ab_recv.at[1])
+    ab[1, a] = s4[1, a]
+    arrived("aback1", ab.at[1], ab_recv.at[1], na - 1)
+    s3[1] = by_ring(split_z, ab[1].reshape(members, HALF))
+    all_z(s3.at[1], zb.at[1], zb_send.at[1], zb_recv.at[1])
+    zb[1, z] = s3[1, z]
+    arrived("zback0", zb.at[0], zb_recv.at[0], nz - 1)
+    s4[0] = by_group(back_z, zb[0].reshape(members, HALF))
+    all_a(s4.at[0], ab.at[0], ab_send.at[0], ab_recv.at[0])
+    ab[0, a] = s4[0, a]
+
+    def put(half, rows):
+        out_ref[:, :, half * HALF : (half + 1) * HALF] = rows.reshape(OWN, patches, HALF)
+
+    arrived("zback1", zb.at[1], zb_recv.at[1], nz - 1)
+    put(1, moved(z_nat[...], zb[1].reshape(members, HALF)))
+    arrived("aback0", ab.at[0], ab_recv.at[0], na - 1)
+    put(0, moved(back_a[...], ab[0].reshape(members, HALF)))
 
     for k in range(chunks):
-        arrived(s1.at[k], a_send.at[k], na - 1)
-        arrived(s2.at[k], z_send.at[k], nz - 1)
-    arrived(s3, zb_send, nz - 1)
-    arrived(s4, ab_send, na - 1)
+        arrived("sent", s1.at[k], a_send.at[k], na - 1)
+        arrived("sent", s2.at[k], z_send.at[k], nz - 1)
+    for half in range(2):
+        arrived("sent", s3.at[half], zb_send.at[half], nz - 1)
+        arrived("sent", s4.at[half], ab_send.at[half], na - 1)
 
 
 def solution(mesh):
@@ -233,37 +283,46 @@
             functools.partial(kernel, nx, nz, nc),
             out_shape=jax.ShapeDtypeStruct(prior_members.shape, bf16),
             in_specs=[
-                pl.BlockSpec(memory_space=pl.ANY),
-                pl.BlockSpec(memory_space=pl.ANY),
-                pl.BlockSpec(memory_space=pltpu.VMEM),
-                pl.BlockSpec(memory_space=pltpu.VMEM),
+                pl.BlockSpec(memory_space=pltpu.HBM),
+                pl.BlockSpec(memory_space=pltpu.HBM),
+                pl.BlockSpec(memory_space=pltpu.HBM),
+                pl.BlockSpec(memory_space=pltpu.HBM),
                 pl.BlockSpec(memory_space=pltpu.SMEM),
             ],
             out_specs=pl.BlockSpec(memory_space=pltpu.VMEM),
             scratch_shapes=[
                 pltpu.VMEM((chunks, members, CHUNK), bf16),
-                perm, perm, perm, perm,
+                pltpu.VMEM(departure.shape, f32),
+                pltpu.VMEM(precision_factor.shape, f32),
+                perm, perm, perm, perm, perm, perm,
                 pltpu.VMEM((chunks, *by_a), bf16),
                 pltpu.VMEM((chunks, *by_a), bf16),
                 pltpu.VMEM((chunks, *by_z), bf16),
                 pltpu.VMEM((chunks, *by_z), bf16),
-                pltpu.VMEM(by_z, bf16),
-                pltpu.VMEM(by_z, bf16),
-                pltpu.VMEM(by_a, bf16),
-                pltpu.VMEM(by_a, bf16),
+                pltpu.VMEM((2, nz, OWN * na, HALF), bf16),
+                pltpu.VMEM((2, nz, OWN * na, HALF), bf16),
+                pltpu.VMEM((2, na, OWN * nz, HALF), bf16),
+                pltpu.VMEM((2, na, OWN * nz, HALF), bf16),
                 square,
                 pltpu.VMEM((members, 1), f32),
                 square,
                 square,
                 dma((chunks, OWN)),
+                dma((2,)),
                 dma((chunks,)), dma((chunks,)),
                 dma((chunks,)), dma((chunks,)),
-                dma, dma, dma, dma,
+                dma((2,)), dma((2,)), dma((2,)), dma((2,)),
             ],
             compiler_params=pltpu.CompilerParams(
                 collective_id=0, has_side_effects=True, vmem_limit_bytes=48 << 20
             ),
-        )(prior_members, mapped_prior, departure, precision_factor, measured_lines)
+        )(
+            *(
+                pltpu.with_memory_space_constraint(array, pltpu.HBM)
+                for array in (prior_members, mapped_prior, departure, precision_factor)
+            ),
+            measured_lines,
+        )
 
     return jax.shard_map(
         local,

time: 71.3 us -> 61.3 us (0.86)
  Pallas kernels: 66.4 us -> 59.8 us
  local copies, waits for them, and re-layouts: 3.97 us -> 0.66 us
    pallas_call x1, Pallas kernels: 66.4 us -> 59.8 us  [local(): pl.pallas_call(functools.partial(kernel, nx, nz, nc), out_shape=jax.Shape...]
    unnamed x9 -> x1, local copies, waits for them, and re-layouts: 3.97 us -> 0.66 us
where the time goes in v2:
time: 61.3 us; the launch traced here: 61.1 us
  Pallas kernels  59.8 us (98%)
  local copies, waits for them, and re-layouts  0.66 us (1%)
  between operations  0.66 us (1%)
    pallas_call x1, Pallas kernels, local(): pl.pallas_call(functools.partial(kernel, nx, nz, nc), out_shape=jax.Shape...  59.8 us

profile of v2, /device:TPU:1, one launch (start us, length us, event | category | flops | bytes accessed | tf_op | source)
XLA Modules:
  0.0 61.1 jit_solution(16798686285157236508)
XLA Ops:
  0.7 59.8 %shard_map.55 = bf16[2,128,256]{2,1,0:T(8,128)(2,1)S(1)} custom-call(bf16[2,128,256]{2,1,0:T(8,128)(2,1)} %prior_hbm.1, bf16[2,128,1024]{2,1,0:T(8,128)(2,1)} %mapped_hbm.1, f32[1,1024]{1,0:T(1,128)} %dep_hbm.1, f32[1,1024]{1,0:T(1,128)} %prec_hbm.1, s32[1]{0:T(128)S(6)} %copy.7.lines_ref), custom_call_target="tpu_custom_call" | custom-call | tf_op jit(solution)/shard_map/pallas_call | solution.py:282
  60.5 0.7 %copy.8 = bf16[2,128,256]{2,1,0:T(8,128)(2,1)} copy(bf16[2,128,256]{2,1,0:T(8,128)(2,1)S(1)} %shard_map.55) | data formatting | bytes 262144

commit v3 on v2

v3 whole, which is shorter than its diff:
```python
import functools
import math

import jax
import jax.numpy as jnp
from jax import lax
from jax.experimental import pallas as pl
from jax.experimental.pallas import tpu as pltpu
from jax.sharding import Mesh
from jax.sharding import PartitionSpec as P

ITERS = 5
OWN = 2
CHUNK = 256
HALF = CHUNK // 2
MEM = ("x", "z", "c")
GRP_MEM = ("grp", "x", "z", "c")
MESH_ID = pl.DeviceIdType.MESH

f32 = jnp.float32
bf16 = jnp.bfloat16


def one_hot(rows, source_of):
    out_row = lax.broadcasted_iota(jnp.int32, (rows, rows), 0)
    in_row = lax.broadcasted_iota(jnp.int32, (rows, rows), 1)
    return jnp.where(in_row == source_of(out_row), f32(1.0), f32(0.0)).astype(bf16)


def moved(perm, rows):
    return jnp.dot(perm, rows, preferred_element_type=f32).astype(bf16)


def halves(value):
    high = value.astype(bf16)
    return high, (value - high.astype(f32)).astype(bf16)


def product(left, right, contract=1, against=0):
    def dot(p, q):
        return lax.dot_general(
            p, q, (((contract,), (against,)), ((), ())), preferred_element_type=f32
        )

    return dot(left[0], right[0]) + (dot(left[0], right[1]) + dot(left[1], right[0]))


def kernel(
    nx, nz, nc,
    prior_hbm, mapped_hbm, dep_hbm, prec_hbm, lines_ref, out_ref,
    raw, dep_ref, prec_ref,
    split_a, split_z, back_z, back_a, nat_z, z_nat,
    s1, ar, s2, zr, s2p, zrp, s3, zb, s4, ab, gram, pull,
    raw_sem, row_sem, far, a_send, a_recv, z_send, z_recv,
    p_send, p_recv, zb_send, zb_recv, ab_send, ab_recv,
):
    na = nx * nc
    members = OWN * na * nz
    obs_chunks = mapped_hbm.shape[2] // CHUNK
    chunks = obs_chunks + 1
    patches = nx * nz * nc
    hop = max(1, 3 * nz // 16)
    near = nz // 2 - hop
    x, z, c = lax.axis_index("x"), lax.axis_index("z"), lax.axis_index("c")
    a = x * nc + c

    barrier = pltpu.get_barrier_semaphore()

    def signal_z(sem, step):
        pl.semaphore_signal(
            sem, inc=1, device_id={"z": lax.rem(z + nz + step, nz)}, device_id_type=MESH_ID
        )

    def greet_z(j, _):
        signal_z(barrier, near - j)
        signal_z(barrier, j - near)
        return 0

    def greet_a(j, _):
        t = lax.rem(a + j, na)
        pl.semaphore_signal(
            barrier, inc=1, device_id={"x": t // nc, "c": lax.rem(t, nc)}, device_id_type=MESH_ID
        )
        return 0

    lax.fori_loop(0, near, greet_z, 0)
    lax.fori_loop(1, na, greet_a, 0)

    def raw_copies(k):
        if k < obs_chunks:
            src = lambda m: mapped_hbm.at[m, :, pl.ds(k * CHUNK, CHUNK)]
        else:
            src = lambda m: prior_hbm.at[m]
        return [
            pltpu.make_async_copy(src(m), raw.at[k, pl.ds(m * patches, patches)], raw_sem.at[k, m])
            for m in range(OWN)
        ]

    row_copies = [
        pltpu.make_async_copy(dep_hbm, dep_ref, row_sem.at[0]),
        pltpu.make_async_copy(prec_hbm, prec_ref, row_sem.at[1]),
    ]
    for k in range(chunks):
        for copy in raw_copies(k):
            copy.start()
    for copy in row_copies:
        copy.start()

    def natural(m, xi, zi, ci):
        return m * patches + xi * (nz * nc) + zi * nc + ci

    def of_natural(r):
        return r // patches, (r // (nz * nc)) % nx, (r // nc) % nz, r % nc

    def of_group(r):
        return r % OWN, r // (OWN * nz * nc), (r // OWN) % nz, (r // (OWN * nz)) % nc

    def of_ring(r):
        return r % OWN, (r // (OWN * nc)) % nx, r // (OWN * na), (r // OWN) % nc

    def group(m, xi, zi, ci):
        return ((xi * nc + ci) * nz + zi) * OWN + m

    def ring(m, xi, zi, ci):
        return ((zi * nx + xi) * nc + ci) * OWN + m

    def a_copy(src, dst, send, recv, j):
        t = lax.rem(a + j, na)
        return pltpu.make_async_remote_copy(
            src_ref=src.at[t], dst_ref=dst.at[a], send_sem=send, recv_sem=recv,
            device_id={"x": t // nc, "c": lax.rem(t, nc)}, device_id_type=MESH_ID,
        )

    def z_copy(src, dst, send, recv, step):
        t = lax.rem(z + nz + step, nz)
        return pltpu.make_async_remote_copy(
            src_ref=src.at[t], dst_ref=dst.at[z], send_sem=send, recv_sem=recv,
            device_id={"z": t}, device_id_type=MESH_ID,
        )

    def all_a(src, dst, send, recv):
        def body(j, _):
            a_copy(src, dst, send, recv, j).start()
            return 0

        lax.fori_loop(1, na, body, 0)

    def ring_steps(most, least, *copy_args):
        def body(j, _):
            z_copy(*copy_args, most - j).start()
            z_copy(*copy_args, j - most).start()
            return 0

        lax.fori_loop(0, most - least + 1, body, 0)

    def opposite(*copy_args):
        z_copy(*copy_args, nz // 2).start()

    def all_z(*copy_args):
        opposite(*copy_args)
        ring_steps(nz // 2 - 1, 1, *copy_args)

    def arrived(name, ref, sem, n):
        part = ref.at[pl.ds(0, n)]
        with jax.named_scope(name):
            pltpu.make_async_copy(part, part, sem).wait()

    def by_group(perm, rows):
        return moved(perm[...], rows).reshape(na, OWN * nz, -1)

    def by_ring(perm, rows):
        return moved(perm[...], rows).reshape(nz, OWN * na, -1)

    def send_group(k):
        for copy in raw_copies(k):
            copy.wait()
        s1[k] = by_group(split_a, raw[k])
        all_a(s1.at[k], ar.at[k], a_send.at[k], a_recv.at[k])
        ar[k, a] = s1[k, a]

    nat_z[...] = one_hot(members, lambda r: natural(*of_ring(r)))
    for copy in raw_copies(0):
        copy.wait()
    s2[0] = by_ring(nat_z, raw[0])
    zr[0, z] = s2[0, z]
    split_a[...] = one_hot(members, lambda r: natural(*of_group(r)))
    first = (s2.at[0], zr.at[0], z_send.at[0], z_recv.at[0])
    with jax.named_scope("greet"):
        pl.semaphore_wait(barrier, 2 * near + na - 1)
    signal_z(far, hop)
    signal_z(far, -hop)
    ring_steps(near, 1, *first)
    for k in range(1, chunks - 2):
        send_group(k)
    with jax.named_scope("far"):
        pl.semaphore_wait(far, 2)
    opposite(*first)
    if near + 1 < nz // 2:
        ring_steps(nz // 2 - 1, near + 1, *first)
    for k in range(chunks - 2, chunks):
        send_group(k)
    split_z[...] = one_hot(members, lambda r: group(*of_ring(r)))
    back_z[...] = one_hot(members, lambda r: ring(*of_group(r)))
    for k in range(1, chunks):
        arrived(f"a{k}", ar.at[k], a_recv.at[k], na - 1)
        rows = ar[k].reshape(members, CHUNK)
        if k < obs_chunks:
            s2[k] = by_ring(split_z, rows)
            all_z(s2.at[k], zr.at[k], z_send.at[k], z_recv.at[k])
            zr[k, z] = s2[k, z]
        else:
            rows = moved(split_z[...], rows)
            for h in range(2):
                s2p[h] = rows[:, h * HALF : (h + 1) * HALF].reshape(nz, OWN * na, HALF)
                all_z(s2p.at[h], zrp.at[h], p_send.at[h], p_recv.at[h])
                zrp[h, z] = s2p[h, z]
    back_a[...] = one_hot(members, lambda r: group(*of_natural(r)))
    z_nat[...] = one_hot(members, lambda r: ring(*of_natural(r)))

    arrived("z0", zr.at[0], z_recv.at[0], nz - 1)
    s1[0] = by_group(back_z, zr[0].reshape(members, CHUNK))
    all_a(s1.at[0], ar.at[0], a_send.at[0], a_recv.at[0])
    ar[0, a] = s1[0, a]

    for copy in row_copies:
        copy.wait()
    lines = lines_ref[0]
    eye = (
        lax.broadcasted_iota(jnp.int32, (members, members), 0)
        == lax.broadcasted_iota(jnp.int32, (members, members), 1)
    )
    gram[...] = jnp.where(eye, f32(members - 1), f32(0.0))
    pull[...] = jnp.zeros_like(pull)
    for k in (*range(1, obs_chunks - 1), 0, obs_chunks - 1):
        if k == 0:
            arrived("a0", ar.at[0], a_recv.at[0], na - 1)
            values = jnp.dot(
                split_z[...], ar[0].reshape(members, CHUNK), preferred_element_type=f32
            )
        else:
            arrived(f"z{k}", zr.at[k], z_recv.at[k], nz - 1)
            values = zr[k].reshape(members, CHUNK).astype(f32)
        with jax.named_scope("gram"):
            deviat = values - jnp.mean(values, axis=0, keepdims=True)
            row_ids = k * CHUNK + lax.broadcasted_iota(jnp.int32, (1, CHUNK), 1)
            cols = pl.ds(k * CHUNK, CHUNK)
            weights = jnp.where(row_ids < lines, prec_ref[:, cols], f32(0.0))
            weighted = deviat * weights
            gram[...] += product(halves(weighted), halves(deviat), 1, 1)
            pull[...] += jnp.sum(weighted * dep_ref[:, cols], axis=1, keepdims=True)

    with jax.named_scope("newton"):
        system = gram[...]
        scale = jnp.sqrt(
            jnp.sum(jnp.sum(system * system, axis=1, keepdims=True), axis=0, keepdims=True)
        )
        identity = jnp.where(eye, f32(1.5), f32(0.0))
        iterate = system / scale
        root = identity - 0.5 * iterate
        factor_halves = halves(root)
        root_halves = factor_halves
        iterate_halves = halves(product(halves(iterate), factor_halves))
        for sweep in range(1, ITERS):
            factor_halves = halves(identity - 0.5 * product(root_halves, iterate_halves))
            root = product(factor_halves, root_halves)
            if sweep < ITERS - 1:
                iterate_halves = halves(product(iterate_halves, factor_halves))
                root_halves = halves(root)

        inner = jnp.sum(root * pull[...], axis=0, keepdims=True)
        shift = jnp.sum(root * inner, axis=1, keepdims=True) / scale
        shift = jnp.sum(jnp.where(eye, shift, f32(0.0)), axis=0, keepdims=True)
        transform = halves((math.sqrt(members - 1) / jnp.sqrt(scale)) * root + shift)

    def result(h):
        arrived(f"p{h}", zrp.at[h], p_recv.at[h], nz - 1)
        quantities = zrp[h].reshape(members, HALF).astype(f32)
        center = jnp.mean(quantities, axis=0, keepdims=True)
        return (center + product(transform, halves(quantities - center))).astype(bf16)

    s3[0] = result(0).reshape(nz, OWN * na, HALF)
    all_z(s3.at[0], zb.at[0], zb_send.at[0], zb_recv.at[0])
    zb[0, z] = s3[0, z]
    s4[1] = by_group(back_z, result(1))
    all_a(s4.at[1], ab.at[1], ab_send.at[1], ab_recv.at[1])
    ab[1, a] = s4[1, a]
    arrived("aback1", ab.at[1], ab_recv.at[1], na - 1)
    s3[1] = by_ring(split_z, ab[1].reshape(members, HALF))
    all_z(s3.at[1], zb.at[1], zb_send.at[1], zb_recv.at[1])
    zb[1, z] = s3[1, z]
    arrived("zback0", zb.at[0], zb_recv.at[0], nz - 1)
    s4[0] = by_group(back_z, zb[0].reshape(members, HALF))
    all_a(s4.at[0], ab.at[0], ab_send.at[0], ab_recv.at[0])
    ab[0, a] = s4[0, a]

    def put(half, rows):
        out_ref[:, :, half * HALF : (half + 1) * HALF] = rows.reshape(OWN, patches, HALF)

    arrived("aback0", ab.at[0], ab_recv.at[0], na - 1)
    put(0, moved(back_a[...], ab[0].reshape(members, HALF)))
    arrived("zback1", zb.at[1], zb_recv.at[1], nz - 1)
    put(1, moved(z_nat[...], zb[1].reshape(members, HALF)))

    for k in range(chunks):
        arrived("sent", s1.at[k], a_send.at[k], na - 1)
        if k < obs_chunks:
            arrived("sent", s2.at[k], z_send.at[k], nz - 1)
    for half in range(2):
        arrived("sent", s2p.at[half], p_send.at[half], nz - 1)
        arrived("sent", s3.at[half], zb_send.at[half], nz - 1)
        arrived("sent", s4.at[half], ab_send.at[half], na - 1)


def solution(mesh):
    nx, nz, nc = 4, 16, 2
    split = Mesh(mesh.devices.reshape(nx, nz, nc, mesh.shape["grp"]), ("x", "z", "c", "grp"))
    na = nx * nc
    members = OWN * na * nz

    def local(prior_members, mapped_prior, departure, precision_factor, measured_lines):
        chunks = mapped_prior.shape[2] // CHUNK + 1
        perm = pltpu.VMEM((members, members), bf16)
        by_a = (na, OWN * nz)
        by_z = (nz, OWN * na)
        dma = pltpu.SemaphoreType.DMA
        return pl.pallas_call(
            functools.partial(kernel, nx, nz, nc),
            out_shape=jax.ShapeDtypeStruct(prior_members.shape, bf16),
            in_specs=[
                pl.BlockSpec(memory_space=pltpu.HBM),
                pl.BlockSpec(memory_space=pltpu.HBM),
                pl.BlockSpec(memory_space=pltpu.HBM),
                pl.BlockSpec(memory_space=pltpu.HBM),
                pl.BlockSpec(memory_space=pltpu.SMEM),
            ],
            out_specs=pl.BlockSpec(memory_space=pltpu.VMEM),
            scratch_shapes=[
                pltpu.VMEM((chunks, members, CHUNK), bf16),
                pltpu.VMEM(departure.shape, f32),
                pltpu.VMEM(precision_factor.shape, f32),
                perm, perm, perm, perm, perm, perm,
                pltpu.VMEM((chunks, *by_a, CHUNK), bf16),
                pltpu.VMEM((chunks, *by_a, CHUNK), bf16),
                pltpu.VMEM((chunks - 1, *by_z, CHUNK), bf16),
                pltpu.VMEM((chunks - 1, *by_z, CHUNK), bf16),
                pltpu.VMEM((2, *by_z, HALF), bf16),
                pltpu.VMEM((2, *by_z, HALF), bf16),
                pltpu.VMEM((2, *by_z, HALF), bf16),
                pltpu.VMEM((2, *by_z, HALF), bf16),
                pltpu.VMEM((2, *by_a, HALF), bf16),
                pltpu.VMEM((2, *by_a, HALF), bf16),
                pltpu.VMEM((members, members), f32),
                pltpu.VMEM((members, 1), f32),
                dma((chunks, OWN)),
                dma((2,)),
                pltpu.SemaphoreType.REGULAR,
                dma((chunks,)), dma((chunks,)),
                dma((chunks - 1,)), dma((chunks - 1,)),
                dma((2,)), dma((2,)),
                dma((2,)), dma((2,)),
                dma((2,)), dma((2,)),
            ],
            compiler_params=pltpu.CompilerParams(
                collective_id=0, has_side_effects=True, vmem_limit_bytes=48 << 20
            ),
        )(
            *(
                pltpu.with_memory_space_constraint(array, pltpu.HBM)
                for array in (
                    prior_members, mapped_prior, departure, precision_factor,
                )
            ),
            measured_lines,
        )

    return jax.shard_map(
        local,
        mesh=split,
        in_specs=(
            P(MEM, "grp", None),
            P(MEM, "grp", None),
            P(GRP_MEM, None),
            P(GRP_MEM, None),
            P(GRP_MEM),
        ),
        out_specs=P(MEM, "grp", None),
        check_vma=False,
    )
```

time: 61.3 us -> 59.6 us (0.972)
  Pallas kernels: 59.8 us -> 58.1 us
    pallas_call x1, Pallas kernels: 59.8 us -> 58.1 us  [local(): pl.pallas_call(functools.partial(kernel, nx, nz, nc), out_shape=jax.Shape...]
where the time goes in v3:
time: 59.6 us; the launch traced here: 59.4 us
  Pallas kernels  58.1 us (97%)
  local copies, waits for them, and re-layouts  0.66 us (1%)
  between operations  0.66 us (1%)
    pallas_call x1, Pallas kernels, local(): pl.pallas_call(functools.partial(kernel, nx, nz, nc), out_shape=jax.Shape...  58.1 us

profile of v3, /device:TPU:1, one launch (start us, length us, event | category | flops | bytes accessed | tf_op | source)
XLA Modules:
  0.0 59.4 jit_solution(9796219326047482546)
XLA Ops:
  0.7 58.1 %shard_map.55 = bf16[2,128,256]{2,1,0:T(8,128)(2,1)S(1)} custom-call(bf16[2,128,256]{2,1,0:T(8,128)(2,1)} %prior_hbm.1, bf16[2,128,1024]{2,1,0:T(8,128)(2,1)} %mapped_hbm.1, f32[1,1024]{1,0:T(1,128)} %dep_hbm.1, f32[1,1024]{1,0:T(1,128)} %prec_hbm.1, s32[1]{0:T(128)S(6)} %copy.7.lines_ref), custom_call_target="tpu_custom_call" | custom-call | tf_op jit(solution)/shard_map/pallas_call | solution.py:326
  58.8 0.7 %copy.8 = bf16[2,128,256]{2,1,0:T(8,128)(2,1)} copy(bf16[2,128,256]{2,1,0:T(8,128)(2,1)S(1)} %shard_map.55) | data formatting | bytes 262144

commit v4 on v3

--- a/solution.py
+++ b/solution.py
@@ -13,6 +13,7 @@
 OWN = 2
 CHUNK = 256
 HALF = CHUNK // 2
+RING_FIRST = 2
 MEM = ("x", "z", "c")
 GRP_MEM = ("grp", "x", "z", "c")
 MESH_ID = pl.DeviceIdType.MESH
@@ -50,17 +51,17 @@
     prior_hbm, mapped_hbm, dep_hbm, prec_hbm, lines_ref, out_ref,
     raw, dep_ref, prec_ref,
     split_a, split_z, back_z, back_a, nat_z, z_nat,
-    s1, ar, s2, zr, s2p, zrp, s3, zb, s4, ab, gram, pull,
+    s1, ar, s2, zr, s2p, zrp, s3, zb, s4, ab, s5, db, gram, pull,
     raw_sem, row_sem, far, a_send, a_recv, z_send, z_recv,
-    p_send, p_recv, zb_send, zb_recv, ab_send, ab_recv,
+    p_send, p_recv, zb_send, zb_recv, ab_send, ab_recv, db_sem,
 ):
     na = nx * nc
     members = OWN * na * nz
     obs_chunks = mapped_hbm.shape[2] // CHUNK
     chunks = obs_chunks + 1
     patches = nx * nz * nc
-    hop = max(1, 3 * nz // 16)
-    near = nz // 2 - hop
+    near = max(1, nz // 4)
+    levels = nz // (2 * near)
     x, z, c = lax.axis_index("x"), lax.axis_index("z"), lax.axis_index("c")
     a = x * nc + c
 
@@ -70,11 +71,6 @@
         pl.semaphore_signal(
             sem, inc=1, device_id={"z": lax.rem(z + nz + step, nz)}, device_id_type=MESH_ID
         )
-
-    def greet_z(j, _):
-        signal_z(barrier, near - j)
-        signal_z(barrier, j - near)
-        return 0
 
     def greet_a(j, _):
         t = lax.rem(a + j, na)
@@ -82,9 +78,6 @@
             barrier, inc=1, device_id={"x": t // nc, "c": lax.rem(t, nc)}, device_id_type=MESH_ID
         )
         return 0
-
-    lax.fori_loop(0, near, greet_z, 0)
-    lax.fori_loop(1, na, greet_a, 0)
 
     def raw_copies(k):
         if k < obs_chunks:
@@ -100,7 +93,13 @@
         pltpu.make_async_copy(dep_hbm, dep_ref, row_sem.at[0]),
         pltpu.make_async_copy(prec_hbm, prec_ref, row_sem.at[1]),
     ]
-    for k in range(chunks):
+    for copy in raw_copies(0):
+        copy.start()
+    for step in range(near, 0, -1):
+        signal_z(barrier, step)
+        signal_z(barrier, -step)
+    lax.fori_loop(1, na, greet_a, 0)
+    for k in range(1, chunks):
         for copy in raw_copies(k):
             copy.start()
     for copy in row_copies:
@@ -153,12 +152,70 @@
 
         lax.fori_loop(0, most - least + 1, body, 0)
 
-    def opposite(*copy_args):
+    def ring_part(level, *copy_args):
+        most = near * (level + 1)
+        if most == nz // 2:
+            z_copy(*copy_args, most).start()
+            most -= 1
+        if most > near * level:
+            ring_steps(most, near * level + 1, *copy_args)
+
+    def all_z(*copy_args):
         z_copy(*copy_args, nz // 2).start()
+        ring_steps(nz // 2 - 1, 1, *copy_args)
+
+    def all_a(src, dst, send, recv):
+        def body(j, _):
+            a_copy(src, dst, send, recv, j).start()
+            return 0
+
+        lax.fori_loop(1, na, body, 0)
+
+    def ring_steps(most, least, *copy_args):
+        def body(j, _):
+            z_copy(*copy_args, most - j).start()
+            z_copy(*copy_args, j - most).start()
+            return 0
+
+        lax.fori_loop(0, most - least + 1, body, 0)
+
+    def ring_part(level, *copy_args):
+        most = near * (level + 1)
+        if most == nz // 2:
+            z_copy(*copy_args, most).start()
+            most -= 1
+        if most > near * level:
+            ring_steps(most, near * level + 1, *copy_args)
 
     def all_z(*copy_args):
-        opposite(*copy_args)
+        z_copy(*copy_args, nz // 2).start()
         ring_steps(nz // 2 - 1, 1, *copy_args)
+
+    first, last = nz // 2 - nz // 8, nz // 2 + nz // 8
+
+    def served_first(src, dst, send, recv):
+        for j in range(last - first + 1):
+            t = nz // 2 + ((j + 1) // 2) * (1 if j % 2 else -1)
+
+            @pl.when(z != t)
+            def _():
+                z_copy(src, dst, send, recv, t - z).start()
+
+    def served_later(*copy_args):
+        def one(step):
+            t = lax.rem(z + nz + step, nz)
+
+            @pl.when(jnp.logical_or(t < first, t > last))
+            def _():
+                z_copy(*copy_args, step).start()
+
+        def body(j, _):
+            one(nz // 2 - 1 - j)
+            one(j - nz // 2 + 1)
+            return 0
+
+        one(nz // 2)
+        lax.fori_loop(0, nz // 2 - 1, body, 0)
 
     def arrived(name, ref, sem, n):
         part = ref.at[pl.ds(0, n)]
@@ -178,35 +235,53 @@
         all_a(s1.at[k], ar.at[k], a_send.at[k], a_recv.at[k])
         ar[k, a] = s1[k, a]
 
+    def send_group(k):
+        for copy in raw_copies(k):
+            copy.wait()
+        s1[k] = by_group(split_a, raw[k])
+        all_a(s1.at[k], ar.at[k], a_send.at[k], a_recv.at[k])
+        ar[k, a] = s1[k, a]
+
+    def ring_args(k):
+        return s2.at[k], zr.at[k], z_send.at[k], z_recv.at[k]
+
+    def make_ring(k):
+        for copy in raw_copies(k):
+            copy.wait()
+        s2[k] = by_ring(nat_z, raw[k])
+        zr[k, z] = s2[k, z]
+
     nat_z[...] = one_hot(members, lambda r: natural(*of_ring(r)))
-    for copy in raw_copies(0):
-        copy.wait()
-    s2[0] = by_ring(nat_z, raw[0])
-    zr[0, z] = s2[0, z]
-    split_a[...] = one_hot(members, lambda r: natural(*of_group(r)))
-    first = (s2.at[0], zr.at[0], z_send.at[0], z_recv.at[0])
+    make_ring(0)
     with jax.named_scope("greet"):
         pl.semaphore_wait(barrier, 2 * near + na - 1)
-    signal_z(far, hop)
-    signal_z(far, -hop)
-    ring_steps(near, 1, *first)
-    for k in range(1, chunks - 2):
-        send_group(k)
-    with jax.named_scope("far"):
-        pl.semaphore_wait(far, 2)
-    opposite(*first)
-    if near + 1 < nz // 2:
-        ring_steps(nz // 2 - 1, near + 1, *first)
-    for k in range(chunks - 2, chunks):
+    for level in range(levels):
+        if level:
+            with jax.named_scope(f"far{level}"):
+                pl.semaphore_wait(far.at[level - 1], 2)
+        if level < levels - 1:
+            signal_z(far.at[level], near)
+            signal_z(far.at[level], -near)
+        ring_part(level, *ring_args(0))
+        if level == 0:
+            for k in range(1, RING_FIRST):
+                make_ring(k)
+                ring_part(0, *ring_args(k))
+            split_a[...] = one_hot(members, lambda r: natural(*of_group(r)))
+        else:
+            for k in range(1, RING_FIRST):
+                ring_part(level, *ring_args(k))
+        if RING_FIRST + level < chunks:
+            send_group(RING_FIRST + level)
+    for k in range(RING_FIRST + levels, chunks):
         send_group(k)
     split_z[...] = one_hot(members, lambda r: group(*of_ring(r)))
-    back_z[...] = one_hot(members, lambda r: ring(*of_group(r)))
-    for k in range(1, chunks):
+    for k in range(RING_FIRST, chunks):
         arrived(f"a{k}", ar.at[k], a_recv.at[k], na - 1)
         rows = ar[k].reshape(members, CHUNK)
         if k < obs_chunks:
             s2[k] = by_ring(split_z, rows)
-            all_z(s2.at[k], zr.at[k], z_send.at[k], z_recv.at[k])
+            all_z(*ring_args(k))
             zr[k, z] = s2[k, z]
         else:
             rows = moved(split_z[...], rows)
@@ -214,13 +289,15 @@
                 s2p[h] = rows[:, h * HALF : (h + 1) * HALF].reshape(nz, OWN * na, HALF)
                 all_z(s2p.at[h], zrp.at[h], p_send.at[h], p_recv.at[h])
                 zrp[h, z] = s2p[h, z]
+    back_z[...] = one_hot(members, lambda r: ring(*of_group(r)))
     back_a[...] = one_hot(members, lambda r: group(*of_natural(r)))
     z_nat[...] = one_hot(members, lambda r: ring(*of_natural(r)))
 
-    arrived("z0", zr.at[0], z_recv.at[0], nz - 1)
-    s1[0] = by_group(back_z, zr[0].reshape(members, CHUNK))
-    all_a(s1.at[0], ar.at[0], a_send.at[0], a_recv.at[0])
-    ar[0, a] = s1[0, a]
+    for k in range(RING_FIRST):
+        arrived(f"z{k}", zr.at[k], z_recv.at[k], nz - 1)
+        s1[k] = by_group(back_z, zr[k].reshape(members, CHUNK))
+        all_a(s1.at[k], ar.at[k], a_send.at[k], a_recv.at[k])
+        ar[k, a] = s1[k, a]
 
     for copy in row_copies:
         copy.wait()
@@ -231,11 +308,11 @@
     )
     gram[...] = jnp.where(eye, f32(members - 1), f32(0.0))
     pull[...] = jnp.zeros_like(pull)
-    for k in (*range(1, obs_chunks - 1), 0, obs_chunks - 1):
-        if k == 0:
-            arrived("a0", ar.at[0], a_recv.at[0], na - 1)
+    for k in (*range(RING_FIRST, obs_chunks - 1), *range(RING_FIRST), obs_chunks - 1):
+        if k < RING_FIRST:
+            arrived(f"a{k}", ar.at[k], a_recv.at[k], na - 1)
             values = jnp.dot(
-                split_z[...], ar[0].reshape(members, CHUNK), preferred_element_type=f32
+                split_z[...], ar[k].reshape(members, CHUNK), preferred_element_type=f32
             )
         else:
             arrived(f"z{k}", zr.at[k], z_recv.at[k], nz - 1)
@@ -270,45 +347,78 @@
         inner = jnp.sum(root * pull[...], axis=0, keepdims=True)
         shift = jnp.sum(root * inner, axis=1, keepdims=True) / scale
         shift = jnp.sum(jnp.where(eye, shift, f32(0.0)), axis=0, keepdims=True)
-        transform = halves((math.sqrt(members - 1) / jnp.sqrt(scale)) * root + shift)
-
-    def result(h):
+        transform = (math.sqrt(members - 1) / jnp.sqrt(scale)) * root + shift
+        transform = halves(transform)
+        kept = 1.0 - jnp.sum(
+            transform[0].astype(f32) + transform[1].astype(f32), axis=1, keepdims=True
+        )
+
+    def result(h, rows, kept):
         arrived(f"p{h}", zrp.at[h], p_recv.at[h], nz - 1)
-        quantities = zrp[h].reshape(members, HALF).astype(f32)
-        center = jnp.mean(quantities, axis=0, keepdims=True)
-        return (center + product(transform, halves(quantities - center))).astype(bf16)
-
-    s3[0] = result(0).reshape(nz, OWN * na, HALF)
-    all_z(s3.at[0], zb.at[0], zb_send.at[0], zb_recv.at[0])
-    zb[0, z] = s3[0, z]
-    s4[1] = by_group(back_z, result(1))
-    all_a(s4.at[1], ab.at[1], ab_send.at[1], ab_recv.at[1])
-    ab[1, a] = s4[1, a]
-    arrived("aback1", ab.at[1], ab_recv.at[1], na - 1)
-    s3[1] = by_ring(split_z, ab[1].reshape(members, HALF))
-    all_z(s3.at[1], zb.at[1], zb_send.at[1], zb_recv.at[1])
-    zb[1, z] = s3[1, z]
+        quantities = zrp[h].reshape(members, HALF)
+        center = jnp.mean(quantities.astype(f32), axis=0, keepdims=True)
+        spread = jnp.dot(rows[0], quantities, preferred_element_type=f32) + (
+            jnp.dot(rows[1], quantities, preferred_element_type=f32)
+        )
+        return (spread + kept * center).astype(bf16)
+
+    def group_back(h):
+        all_a(s4.at[h], ab.at[h], ab_send.at[h], ab_recv.at[h])
+        ab[h, a] = s4[h, a]
+
+    def ring_back(h):
+        all_z(s3.at[h], zb.at[h], zb_send.at[h], zb_recv.at[h])
+        zb[h, z] = s3[h, z]
+
+    def put(h, rows):
+        out_ref[:, :, h * HALF : (h + 1) * HALF] = rows.reshape(OWN, patches, HALF)
+
+    s3[0] = result(0, transform, kept).reshape(nz, OWN * na, HALF)
+    ring_back(0)
+    s5[...] = result(1, transform, kept).reshape(s5.shape)
+
+    def straight(step):
+        t = lax.rem(z + nz + step, nz)
+        for j in range(na):
+            g = lax.rem(a + j, na)
+
+            def send():
+                pltpu.make_async_remote_copy(
+                    src_ref=s5.at[t * na + g], dst_ref=db.at[z * na + a],
+                    send_sem=db_sem.at[0], recv_sem=db_sem.at[1],
+                    device_id={"x": g // nc, "z": t, "c": lax.rem(g, nc)},
+                    device_id_type=MESH_ID,
+                ).start()
+
+            if j or not isinstance(step, int) or step:
+                send()
+
+    def straight_both(j, _):
+        straight(nz // 2 - 1 - j)
+        straight(j - nz // 2 + 1)
+        return 0
+
+    straight(nz // 2)
+    lax.fori_loop(0, nz // 2 - 1, straight_both, 0)
+    straight(0)
+    db[z * na + a] = s5[z * na + a]
     arrived("zback0", zb.at[0], zb_recv.at[0], nz - 1)
     s4[0] = by_group(back_z, zb[0].reshape(members, HALF))
-    all_a(s4.at[0], ab.at[0], ab_send.at[0], ab_recv.at[0])
-    ab[0, a] = s4[0, a]
-
-    def put(half, rows):
-        out_ref[:, :, half * HALF : (half + 1) * HALF] = rows.reshape(OWN, patches, HALF)
-
+    group_back(0)
+    arrived("straight", db, db_sem.at[1], na * nz - 1)
+    put(1, moved(z_nat[...], db[...].reshape(members, HALF)))
     arrived("aback0", ab.at[0], ab_recv.at[0], na - 1)
     put(0, moved(back_a[...], ab[0].reshape(members, HALF)))
-    arrived("zback1", zb.at[1], zb_recv.at[1], nz - 1)
-    put(1, moved(z_nat[...], zb[1].reshape(members, HALF)))
+    arrived("sent", s5, db_sem.at[0], na * nz - 1)
 
     for k in range(chunks):
         arrived("sent", s1.at[k], a_send.at[k], na - 1)
         if k < obs_chunks:
             arrived("sent", s2.at[k], z_send.at[k], nz - 1)
+    arrived("sent", s3.at[0], zb_send.at[0], nz - 1)
+    arrived("sent", s4.at[0], ab_send.at[0], na - 1)
     for half in range(2):
         arrived("sent", s2p.at[half], p_send.at[half], nz - 1)
-        arrived("sent", s3.at[half], zb_send.at[half], nz - 1)
-        arrived("sent", s4.at[half], ab_send.at[half], na - 1)
 
 
 def solution(mesh):
@@ -345,20 +455,23 @@
                 pltpu.VMEM((chunks - 1, *by_z, CHUNK), bf16),
                 pltpu.VMEM((2, *by_z, HALF), bf16),
                 pltpu.VMEM((2, *by_z, HALF), bf16),
-                pltpu.VMEM((2, *by_z, HALF), bf16),
-                pltpu.VMEM((2, *by_z, HALF), bf16),
-                pltpu.VMEM((2, *by_a, HALF), bf16),
-                pltpu.VMEM((2, *by_a, HALF), bf16),
+                pltpu.VMEM((1, *by_z, HALF), bf16),
+                pltpu.VMEM((1, *by_z, HALF), bf16),
+                pltpu.VMEM((1, *by_a, HALF), bf16),
+                pltpu.VMEM((1, *by_a, HALF), bf16),
+                pltpu.VMEM((na * nz, OWN, HALF), bf16),
+                pltpu.VMEM((na * nz, OWN, HALF), bf16),
                 pltpu.VMEM((members, members), f32),
                 pltpu.VMEM((members, 1), f32),
                 dma((chunks, OWN)),
                 dma((2,)),
-                pltpu.SemaphoreType.REGULAR,
+                pltpu.SemaphoreType.REGULAR((3,)),
                 dma((chunks,)), dma((chunks,)),
                 dma((chunks - 1,)), dma((chunks - 1,)),
                 dma((2,)), dma((2,)),
-                dma((2,)), dma((2,)),
-                dma((2,)), dma((2,)),
+                dma((1,)), dma((1,)),
+                dma((1,)), dma((1,)),
+                dma((2,)),
             ],
             compiler_params=pltpu.CompilerParams(
                 collective_id=0, has_side_effects=True, vmem_limit_bytes=48 << 20

time: 59.6 us -> 57.5 us (0.965)
  Pallas kernels: 58.1 us -> 56 us
    pallas_call x1, Pallas kernels: 58.1 us -> 56 us  [local(): pl.pallas_call(functools.partial(kernel, nx, nz, nc), out_shape=jax.Shape...]
where the time goes in v4:
time: 57.5 us; the launch traced here: 57.3 us
  Pallas kernels  56 us (97%)
  local copies, waits for them, and re-layouts  0.66 us (1%)
  between operations  0.66 us (1%)
    pallas_call x1, Pallas kernels, local(): pl.pallas_call(functools.partial(kernel, nx, nz, nc), out_shape=jax.Shape...  56 us

profile of v4, /device:TPU:1, one launch (start us, length us, event | category | flops | bytes accessed | tf_op | source)
XLA Modules:
  0.0 57.3 jit_solution(3492295330783560585)
XLA Ops:
  0.7 56.0 %shard_map.55 = bf16[2,128,256]{2,1,0:T(8,128)(2,1)S(1)} custom-call(bf16[2,128,256]{2,1,0:T(8,128)(2,1)} %prior_hbm.1, bf16[2,128,1024]{2,1,0:T(8,128)(2,1)} %mapped_hbm.1, f32[1,1024]{1,0:T(1,128)} %dep_hbm.1, f32[1,1024]{1,0:T(1,128)} %prec_hbm.1, s32[1]{0:T(128)S(6)} %copy.7.lines_ref), custom_call_target="tpu_custom_call" | custom-call | tf_op jit(solution)/shard_map/pallas_call | solution.py:436
  56.6 0.7 %copy.8 = bf16[2,128,256]{2,1,0:T(8,128)(2,1)} copy(bf16[2,128,256]{2,1,0:T(8,128)(2,1)S(1)} %shard_map.55) | data formatting | bytes 262144

commit v5 on v4

--- a/solution.py
+++ b/solution.py
@@ -14,6 +14,7 @@
 CHUNK = 256
 HALF = CHUNK // 2
 RING_FIRST = 2
+NEAR = 4
 MEM = ("x", "z", "c")
 GRP_MEM = ("grp", "x", "z", "c")
 MESH_ID = pl.DeviceIdType.MESH
@@ -50,18 +51,18 @@
     nx, nz, nc,
     prior_hbm, mapped_hbm, dep_hbm, prec_hbm, lines_ref, out_ref,
     raw, dep_ref, prec_ref,
-    split_a, split_z, back_z, back_a, nat_z, z_nat,
-    s1, ar, s2, zr, s2p, zrp, s3, zb, s4, ab, s5, db, gram, pull,
+    split_a, split_z, back_z, nat_z, z_nat,
+    s1, ar, s2, zr, s2p, zrp, s5, db, gram, pull,
     raw_sem, row_sem, far, a_send, a_recv, z_send, z_recv,
-    p_send, p_recv, zb_send, zb_recv, ab_send, ab_recv, db_sem,
+    p_send, p_recv, db_send, db_recv,
 ):
     na = nx * nc
     members = OWN * na * nz
     obs_chunks = mapped_hbm.shape[2] // CHUNK
     chunks = obs_chunks + 1
     patches = nx * nz * nc
-    near = max(1, nz // 4)
-    levels = nz // (2 * near)
+    near = nz * NEAR // 16
+    hop = nz // 2 - near
     x, z, c = lax.axis_index("x"), lax.axis_index("z"), lax.axis_index("c")
     a = x * nc + c
 
@@ -152,6 +153,30 @@
 
         lax.fori_loop(0, most - least + 1, body, 0)
 
+    def ring_far(*copy_args):
+        z_copy(*copy_args, nz // 2).start()
+        if near + 1 < nz // 2:
+            ring_steps(nz // 2 - 1, near + 1, *copy_args)
+
+    def all_z(*copy_args):
+        z_copy(*copy_args, nz // 2).start()
+        ring_steps(nz // 2 - 1, 1, *copy_args)
+
+    def all_a(src, dst, send, recv):
+        def body(j, _):
+            a_copy(src, dst, send, recv, j).start()
+            return 0
+
+        lax.fori_loop(1, na, body, 0)
+
+    def ring_steps(most, least, *copy_args):
+        def body(j, _):
+            z_copy(*copy_args, most - j).start()
+            z_copy(*copy_args, j - most).start()
+            return 0
+
+        lax.fori_loop(0, most - least + 1, body, 0)
+
     def ring_part(level, *copy_args):
         most = near * (level + 1)
         if most == nz // 2:
@@ -164,33 +189,6 @@
         z_copy(*copy_args, nz // 2).start()
         ring_steps(nz // 2 - 1, 1, *copy_args)
 
-    def all_a(src, dst, send, recv):
-        def body(j, _):
-            a_copy(src, dst, send, recv, j).start()
-            return 0
-
-        lax.fori_loop(1, na, body, 0)
-
-    def ring_steps(most, least, *copy_args):
-        def body(j, _):
-            z_copy(*copy_args, most - j).start()
-            z_copy(*copy_args, j - most).start()
-            return 0
-
-        lax.fori_loop(0, most - least + 1, body, 0)
-
-    def ring_part(level, *copy_args):
-        most = near * (level + 1)
-        if most == nz // 2:
-            z_copy(*copy_args, most).start()
-            most -= 1
-        if most > near * level:
-            ring_steps(most, near * level + 1, *copy_args)
-
-    def all_z(*copy_args):
-        z_copy(*copy_args, nz // 2).start()
-        ring_steps(nz // 2 - 1, 1, *copy_args)
-
     first, last = nz // 2 - nz // 8, nz // 2 + nz // 8
 
     def served_first(src, dst, send, recv):
@@ -255,25 +253,19 @@
     make_ring(0)
     with jax.named_scope("greet"):
         pl.semaphore_wait(barrier, 2 * near + na - 1)
-    for level in range(levels):
-        if level:
-            with jax.named_scope(f"far{level}"):
-                pl.semaphore_wait(far.at[level - 1], 2)
-        if level < levels - 1:
-            signal_z(far.at[level], near)
-            signal_z(far.at[level], -near)
-        ring_part(level, *ring_args(0))
-        if level == 0:
-            for k in range(1, RING_FIRST):
-                make_ring(k)
-                ring_part(0, *ring_args(k))
-            split_a[...] = one_hot(members, lambda r: natural(*of_group(r)))
-        else:
-            for k in range(1, RING_FIRST):
-                ring_part(level, *ring_args(k))
-        if RING_FIRST + level < chunks:
-            send_group(RING_FIRST + level)
-    for k in range(RING_FIRST + levels, chunks):
+    signal_z(far, hop)
+    signal_z(far, -hop)
+    ring_steps(near, 1, *ring_args(0))
+    for k in range(1, RING_FIRST):
+        make_ring(k)
+        ring_steps(near, 1, *ring_args(k))
+    split_a[...] = one_hot(members, lambda r: natural(*of_group(r)))
+    send_group(RING_FIRST)
+    with jax.named_scope("far"):
+        pl.semaphore_wait(far, 2)
+    for k in range(RING_FIRST):
+        ring_far(*ring_args(k))
+    for k in range(RING_FIRST + 1, chunks):
         send_group(k)
     split_z[...] = one_hot(members, lambda r: group(*of_ring(r)))
     for k in range(RING_FIRST, chunks):
@@ -290,7 +282,6 @@
                 all_z(s2p.at[h], zrp.at[h], p_send.at[h], p_recv.at[h])
                 zrp[h, z] = s2p[h, z]
     back_z[...] = one_hot(members, lambda r: ring(*of_group(r)))
-    back_a[...] = one_hot(members, lambda r: group(*of_natural(r)))
     z_nat[...] = one_hot(members, lambda r: ring(*of_natural(r)))
 
     for k in range(RING_FIRST):
@@ -362,61 +353,41 @@
         )
         return (spread + kept * center).astype(bf16)
 
-    def group_back(h):
-        all_a(s4.at[h], ab.at[h], ab_send.at[h], ab_recv.at[h])
-        ab[h, a] = s4[h, a]
-
-    def ring_back(h):
-        all_z(s3.at[h], zb.at[h], zb_send.at[h], zb_recv.at[h])
-        zb[h, z] = s3[h, z]
-
-    def put(h, rows):
+    for h in range(2):
+        s5[h] = result(h, transform, kept).reshape(s5.shape[1:])
+
+        def straight(step):
+            t = lax.rem(z + nz + step, nz)
+            for j in range(na):
+                g = lax.rem(a + j, na)
+                if j or not isinstance(step, int) or step:
+                    pltpu.make_async_remote_copy(
+                        src_ref=s5.at[h, t * na + g], dst_ref=db.at[h, z * na + a],
+                        send_sem=db_send.at[h], recv_sem=db_recv.at[h],
+                        device_id={"x": g // nc, "z": t, "c": lax.rem(g, nc)},
+                        device_id_type=MESH_ID,
+                    ).start()
+
+        def straight_both(j, _):
+            straight(nz // 2 - 1 - j)
+            straight(j - nz // 2 + 1)
+            return 0
+
+        straight(nz // 2)
+        lax.fori_loop(0, nz // 2 - 1, straight_both, 0)
+        straight(0)
+        db[h, z * na + a] = s5[h, z * na + a]
+    for h in range(2):
+        arrived(f"straight{h}", db.at[h], db_recv.at[h], na * nz - 1)
+        rows = moved(z_nat[...], db[h].reshape(members, HALF))
         out_ref[:, :, h * HALF : (h + 1) * HALF] = rows.reshape(OWN, patches, HALF)
-
-    s3[0] = result(0, transform, kept).reshape(nz, OWN * na, HALF)
-    ring_back(0)
-    s5[...] = result(1, transform, kept).reshape(s5.shape)
-
-    def straight(step):
-        t = lax.rem(z + nz + step, nz)
-        for j in range(na):
-            g = lax.rem(a + j, na)
-
-            def send():
-                pltpu.make_async_remote_copy(
-                    src_ref=s5.at[t * na + g], dst_ref=db.at[z * na + a],
-                    send_sem=db_sem.at[0], recv_sem=db_sem.at[1],
-                    device_id={"x": g // nc, "z": t, "c": lax.rem(g, nc)},
-                    device_id_type=MESH_ID,
-                ).start()
-
-            if j or not isinstance(step, int) or step:
-                send()
-
-    def straight_both(j, _):
-        straight(nz // 2 - 1 - j)
-        straight(j - nz // 2 + 1)
-        return 0
-
-    straight(nz // 2)
-    lax.fori_loop(0, nz // 2 - 1, straight_both, 0)
-    straight(0)
-    db[z * na + a] = s5[z * na + a]
-    arrived("zback0", zb.at[0], zb_recv.at[0], nz - 1)
-    s4[0] = by_group(back_z, zb[0].reshape(members, HALF))
-    group_back(0)
-    arrived("straight", db, db_sem.at[1], na * nz - 1)
-    put(1, moved(z_nat[...], db[...].reshape(members, HALF)))
-    arrived("aback0", ab.at[0], ab_recv.at[0], na - 1)
-    put(0, moved(back_a[...], ab[0].reshape(members, HALF)))
-    arrived("sent", s5, db_sem.at[0], na * nz - 1)
+    for h in range(2):
+        arrived("sent", s5.at[h], db_send.at[h], na * nz - 1)
 
     for k in range(chunks):
         arrived("sent", s1.at[k], a_send.at[k], na - 1)
         if k < obs_chunks:
             arrived("sent", s2.at[k], z_send.at[k], nz - 1)
-    arrived("sent", s3.at[0], zb_send.at[0], nz - 1)
-    arrived("sent", s4.at[0], ab_send.at[0], na - 1)
     for half in range(2):
         arrived("sent", s2p.at[half], p_send.at[half], nz - 1)
 
@@ -448,30 +419,24 @@
                 pltpu.VMEM((chunks, members, CHUNK), bf16),
                 pltpu.VMEM(departure.shape, f32),
                 pltpu.VMEM(precision_factor.shape, f32),
-                perm, perm, perm, perm, perm, perm,
+                perm, perm, perm, perm, perm,
                 pltpu.VMEM((chunks, *by_a, CHUNK), bf16),
                 pltpu.VMEM((chunks, *by_a, CHUNK), bf16),
                 pltpu.VMEM((chunks - 1, *by_z, CHUNK), bf16),
                 pltpu.VMEM((chunks - 1, *by_z, CHUNK), bf16),
                 pltpu.VMEM((2, *by_z, HALF), bf16),
                 pltpu.VMEM((2, *by_z, HALF), bf16),
-                pltpu.VMEM((1, *by_z, HALF), bf16),
-                pltpu.VMEM((1, *by_z, HALF), bf16),
-                pltpu.VMEM((1, *by_a, HALF), bf16),
-                pltpu.VMEM((1, *by_a, HALF), bf16),
-                pltpu.VMEM((na * nz, OWN, HALF), bf16),
-                pltpu.VMEM((na * nz, OWN, HALF), bf16),
+                pltpu.VMEM((2, na * nz, OWN, HALF), bf16),
+                pltpu.VMEM((2, na * nz, OWN, HALF), bf16),
                 pltpu.VMEM((members, members), f32),
                 pltpu.VMEM((members, 1), f32),
                 dma((chunks, OWN)),
                 dma((2,)),
-                pltpu.SemaphoreType.REGULAR((3,)),
+                pltpu.SemaphoreType.REGULAR,
                 dma((chunks,)), dma((chunks,)),
                 dma((chunks - 1,)), dma((chunks - 1,)),
                 dma((2,)), dma((2,)),
-                dma((1,)), dma((1,)),
-                dma((1,)), dma((1,)),
-                dma((2,)),
+                dma((2,)), dma((2,)),
             ],
             compiler_params=pltpu.CompilerParams(
                 collective_id=0, has_side_effects=True, vmem_limit_bytes=48 << 20

time: 57.5 us -> 56.5 us (0.983)
  Pallas kernels: 56 us -> 55 us
    pallas_call x1, Pallas kernels: 56 us -> 55 us  [local(): pl.pallas_call(functools.partial(kernel, nx, nz, nc), out_shape=jax.Shape...]
where the time goes in v5:
time: 56.5 us; the launch traced here: 56.4 us
  Pallas kernels  55 us (97%)
  local copies, waits for them, and re-layouts  0.66 us (1%)
  between operations  0.66 us (1%)
    pallas_call x1, Pallas kernels, local(): pl.pallas_call(functools.partial(kernel, nx, nz, nc), out_shape=jax.Shape...  55 us

profile of v5, /device:TPU:1, one launch (start us, length us, event | category | flops | bytes accessed | tf_op | source)
XLA Modules:
  0.0 56.4 jit_solution(10174190000424085061)
XLA Ops:
  0.7 55.0 %shard_map.55 = bf16[2,128,256]{2,1,0:T(8,128)(2,1)S(1)} custom-call(bf16[2,128,256]{2,1,0:T(8,128)(2,1)} %prior_hbm.1, bf16[2,128,1024]{2,1,0:T(8,128)(2,1)} %mapped_hbm.1, f32[1,1024]{1,0:T(1,128)} %dep_hbm.1, f32[1,1024]{1,0:T(1,128)} %prec_hbm.1, s32[1]{0:T(128)S(6)} %copy.7.lines_ref), custom_call_target="tpu_custom_call" | custom-call | tf_op jit(solution)/shard_map/pallas_call | solution.py:407
  55.7 0.7 %copy.8 = bf16[2,128,256]{2,1,0:T(8,128)(2,1)} copy(bf16[2,128,256]{2,1,0:T(8,128)(2,1)S(1)} %shard_map.55) | data formatting | bytes 262144

commit v6 on v5

--- a/solution.py
+++ b/solution.py
@@ -12,7 +12,8 @@
 ITERS = 5
 OWN = 2
 CHUNK = 256
-HALF = CHUNK // 2
+HALF = CHUNK
+PIECES = CHUNK // HALF
 RING_FIRST = 2
 NEAR = 4
 MEM = ("x", "z", "c")
@@ -277,7 +278,7 @@
             zr[k, z] = s2[k, z]
         else:
             rows = moved(split_z[...], rows)
-            for h in range(2):
+            for h in range(PIECES):
                 s2p[h] = rows[:, h * HALF : (h + 1) * HALF].reshape(nz, OWN * na, HALF)
                 all_z(s2p.at[h], zrp.at[h], p_send.at[h], p_recv.at[h])
                 zrp[h, z] = s2p[h, z]
@@ -339,22 +340,19 @@
         shift = jnp.sum(root * inner, axis=1, keepdims=True) / scale
         shift = jnp.sum(jnp.where(eye, shift, f32(0.0)), axis=0, keepdims=True)
         transform = (math.sqrt(members - 1) / jnp.sqrt(scale)) * root + shift
-        transform = halves(transform)
-        kept = 1.0 - jnp.sum(
-            transform[0].astype(f32) + transform[1].astype(f32), axis=1, keepdims=True
-        )
-
-    def result(h, rows, kept):
+        kept = 1.0 - jnp.sum(transform, axis=1, keepdims=True)
+        transform = halves(transform + kept / members)
+
+    def result(h):
         arrived(f"p{h}", zrp.at[h], p_recv.at[h], nz - 1)
         quantities = zrp[h].reshape(members, HALF)
-        center = jnp.mean(quantities.astype(f32), axis=0, keepdims=True)
-        spread = jnp.dot(rows[0], quantities, preferred_element_type=f32) + (
-            jnp.dot(rows[1], quantities, preferred_element_type=f32)
-        )
-        return (spread + kept * center).astype(bf16)
-
-    for h in range(2):
-        s5[h] = result(h, transform, kept).reshape(s5.shape[1:])
+        return (
+            jnp.dot(transform[0], quantities, preferred_element_type=f32)
+            + jnp.dot(transform[1], quantities, preferred_element_type=f32)
+        ).astype(bf16)
+
+    for h in range(PIECES):
+        s5[h] = result(h).reshape(s5.shape[1:])
 
         def straight(step):
             t = lax.rem(z + nz + step, nz)
@@ -377,18 +375,18 @@
         lax.fori_loop(0, nz // 2 - 1, straight_both, 0)
         straight(0)
         db[h, z * na + a] = s5[h, z * na + a]
-    for h in range(2):
+    for h in range(PIECES):
         arrived(f"straight{h}", db.at[h], db_recv.at[h], na * nz - 1)
         rows = moved(z_nat[...], db[h].reshape(members, HALF))
         out_ref[:, :, h * HALF : (h + 1) * HALF] = rows.reshape(OWN, patches, HALF)
-    for h in range(2):
+    for h in range(PIECES):
         arrived("sent", s5.at[h], db_send.at[h], na * nz - 1)
 
     for k in range(chunks):
         arrived("sent", s1.at[k], a_send.at[k], na - 1)
         if k < obs_chunks:
             arrived("sent", s2.at[k], z_send.at[k], nz - 1)
-    for half in range(2):
+    for half in range(PIECES):
         arrived("sent", s2p.at[half], p_send.at[half], nz - 1)
 
 
@@ -424,10 +422,10 @@
                 pltpu.VMEM((chunks, *by_a, CHUNK), bf16),
                 pltpu.VMEM((chunks - 1, *by_z, CHUNK), bf16),
                 pltpu.VMEM((chunks - 1, *by_z, CHUNK), bf16),
-                pltpu.VMEM((2, *by_z, HALF), bf16),
-                pltpu.VMEM((2, *by_z, HALF), bf16),
-                pltpu.VMEM((2, na * nz, OWN, HALF), bf16),
-                pltpu.VMEM((2, na * nz, OWN, HALF), bf16),
+                pltpu.VMEM((PIECES, *by_z, HALF), bf16),
+                pltpu.VMEM((PIECES, *by_z, HALF), bf16),
+                pltpu.VMEM((PIECES, na * nz, OWN, HALF), bf16),
+                pltpu.VMEM((PIECES, na * nz, OWN, HALF), bf16),
                 pltpu.VMEM((members, members), f32),
                 pltpu.VMEM((members, 1), f32),
                 dma((chunks, OWN)),

time: 56.5 us -> 55.5 us (0.982)
  Pallas kernels: 55 us -> 54.1 us
    pallas_call x1, Pallas kernels: 55 us -> 54.1 us  [local(): pl.pallas_call(functools.partial(kernel, nx, nz, nc), out_shape=jax.Shape...]
where the time goes in v6:
time: 55.5 us; the launch traced here: 55.4 us
  Pallas kernels  54.1 us (97%)
  local copies, waits for them, and re-layouts  0.66 us (1%)
  between operations  0.66 us (1%)
    pallas_call x1, Pallas kernels, local(): pl.pallas_call(functools.partial(kernel, nx, nz, nc), out_shape=jax.Shape...  54.1 us

profile of v6, /device:TPU:1, one launch (start us, length us, event | category | flops | bytes accessed | tf_op | source)
XLA Modules:
  0.0 55.4 jit_solution(4224395269072568662)
XLA Ops:
  0.7 54.1 %shard_map.55 = bf16[2,128,256]{2,1,0:T(8,128)(2,1)S(1)} custom-call(bf16[2,128,256]{2,1,0:T(8,128)(2,1)} %prior_hbm.1, bf16[2,128,1024]{2,1,0:T(8,128)(2,1)} %mapped_hbm.1, f32[1,1024]{1,0:T(1,128)} %dep_hbm.1, f32[1,1024]{1,0:T(1,128)} %prec_hbm.1, s32[1]{0:T(128)S(6)} %copy.7.lines_ref), custom_call_target="tpu_custom_call" | custom-call | tf_op jit(solution)/shard_map/pallas_call | solution.py:405
  54.7 0.7 %copy.8 = bf16[2,128,256]{2,1,0:T(8,128)(2,1)} copy(bf16[2,128,256]{2,1,0:T(8,128)(2,1)S(1)} %shard_map.55) | data formatting | bytes 262144

commit v7 on v6

--- a/solution.py
+++ b/solution.py
@@ -87,7 +87,7 @@
         else:
             src = lambda m: prior_hbm.at[m]
         return [
-            pltpu.make_async_copy(src(m), raw.at[k, pl.ds(m * patches, patches)], raw_sem.at[k, m])
+            pltpu.make_async_copy(src(m), raw.at[k, pl.ds(m * patches, patches)], raw_sem.at[k])
             for m in range(OWN)
         ]
 
@@ -125,12 +125,11 @@
     def ring(m, xi, zi, ci):
         return ((zi * nx + xi) * nc + ci) * OWN + m
 
-    def a_copy(src, dst, send, recv, j):
-        t = lax.rem(a + j, na)
-        return pltpu.make_async_remote_copy(
-            src_ref=src.at[t], dst_ref=dst.at[a], send_sem=send, recv_sem=recv,
-            device_id={"x": t // nc, "c": lax.rem(t, nc)}, device_id_type=MESH_ID,
-        )
+    columns = [
+        (lax.rem(x + dx, nx), lax.rem(c + dc, nc))
+        for dx in sorted(range(nx), key=lambda d: -min(d, nx - d))
+        for dc in range(nc - 1, -1, -1)
+    ]
 
     def z_copy(src, dst, send, recv, step):
         t = lax.rem(z + nz + step, nz)
@@ -140,11 +139,11 @@
         )
 
     def all_a(src, dst, send, recv):
-        def body(j, _):
-            a_copy(src, dst, send, recv, j).start()
-            return 0
-
-        lax.fori_loop(1, na, body, 0)
+        for to_x, to_c in columns[:-1]:
+            pltpu.make_async_remote_copy(
+                src_ref=src.at[to_x * nc + to_c], dst_ref=dst.at[a], send_sem=send, recv_sem=recv,
+                device_id={"x": to_x, "c": to_c}, device_id_type=MESH_ID,
+            ).start()
 
     def ring_steps(most, least, *copy_args):
         def body(j, _):
@@ -163,59 +162,6 @@
         z_copy(*copy_args, nz // 2).start()
         ring_steps(nz // 2 - 1, 1, *copy_args)
 
-    def all_a(src, dst, send, recv):
-        def body(j, _):
-            a_copy(src, dst, send, recv, j).start()
-            return 0
-
-        lax.fori_loop(1, na, body, 0)
-
-    def ring_steps(most, least, *copy_args):
-        def body(j, _):
-            z_copy(*copy_args, most - j).start()
-            z_copy(*copy_args, j - most).start()
-            return 0
-
-        lax.fori_loop(0, most - least + 1, body, 0)
-
-    def ring_part(level, *copy_args):
-        most = near * (level + 1)
-        if most == nz // 2:
-            z_copy(*copy_args, most).start()
-            most -= 1
-        if most > near * level:
-            ring_steps(most, near * level + 1, *copy_args)
-
-    def all_z(*copy_args):
-        z_copy(*copy_args, nz // 2).start()
-        ring_steps(nz // 2 - 1, 1, *copy_args)
-
-    first, last = nz // 2 - nz // 8, nz // 2 + nz // 8
-
-    def served_first(src, dst, send, recv):
-        for j in range(last - first + 1):
-            t = nz // 2 + ((j + 1) // 2) * (1 if j % 2 else -1)
-
-            @pl.when(z != t)
-            def _():
-                z_copy(src, dst, send, recv, t - z).start()
-
-    def served_later(*copy_args):
-        def one(step):
-            t = lax.rem(z + nz + step, nz)
-
-            @pl.when(jnp.logical_or(t < first, t > last))
-            def _():
-                z_copy(*copy_args, step).start()
-
-        def body(j, _):
-            one(nz // 2 - 1 - j)
-            one(j - nz // 2 + 1)
-            return 0
-
-        one(nz // 2)
-        lax.fori_loop(0, nz // 2 - 1, body, 0)
-
     def arrived(name, ref, sem, n):
         part = ref.at[pl.ds(0, n)]
         with jax.named_scope(name):
@@ -228,25 +174,16 @@
         return moved(perm[...], rows).reshape(nz, OWN * na, -1)
 
     def send_group(k):
-        for copy in raw_copies(k):
-            copy.wait()
+        pltpu.make_async_copy(raw.at[k], raw.at[k], raw_sem.at[k]).wait()
         s1[k] = by_group(split_a, raw[k])
-        all_a(s1.at[k], ar.at[k], a_send.at[k], a_recv.at[k])
+        all_a(s1.at[k], ar.at[k], a_send, a_recv.at[k])
         ar[k, a] = s1[k, a]
 
-    def send_group(k):
-        for copy in raw_copies(k):
-            copy.wait()
-        s1[k] = by_group(split_a, raw[k])
-        all_a(s1.at[k], ar.at[k], a_send.at[k], a_recv.at[k])
-        ar[k, a] = s1[k, a]
-
     def ring_args(k):
-        return s2.at[k], zr.at[k], z_send.at[k], z_recv.at[k]
+        return s2.at[k], zr.at[k], z_send, z_recv.at[k]
 
     def make_ring(k):
-        for copy in raw_copies(k):
-            copy.wait()
+        pltpu.make_async_copy(raw.at[k], raw.at[k], raw_sem.at[k]).wait()
         s2[k] = by_ring(nat_z, raw[k])
         zr[k, z] = s2[k, z]
 
@@ -288,7 +225,7 @@
     for k in range(RING_FIRST):
         arrived(f"z{k}", zr.at[k], z_recv.at[k], nz - 1)
         s1[k] = by_group(back_z, zr[k].reshape(members, CHUNK))
-        all_a(s1.at[k], ar.at[k], a_send.at[k], a_recv.at[k])
+        all_a(s1.at[k], ar.at[k], a_send, a_recv.at[k])
         ar[k, a] = s1[k, a]
 
     for copy in row_copies:
@@ -356,15 +293,13 @@
 
         def straight(step):
             t = lax.rem(z + nz + step, nz)
-            for j in range(na):
-                g = lax.rem(a + j, na)
-                if j or not isinstance(step, int) or step:
-                    pltpu.make_async_remote_copy(
-                        src_ref=s5.at[h, t * na + g], dst_ref=db.at[h, z * na + a],
-                        send_sem=db_send.at[h], recv_sem=db_recv.at[h],
-                        device_id={"x": g // nc, "z": t, "c": lax.rem(g, nc)},
-                        device_id_type=MESH_ID,
-                    ).start()
+            own = isinstance(step, int) and step == 0
+            for to_x, to_c in columns[:-1] if own else columns:
+                pltpu.make_async_remote_copy(
+                    src_ref=s5.at[h, (t * nx + to_x) * nc + to_c], dst_ref=db.at[h, z * na + a],
+                    send_sem=db_send.at[h], recv_sem=db_recv.at[h],
+                    device_id={"x": to_x, "z": t, "c": to_c}, device_id_type=MESH_ID,
+                ).start()
 
         def straight_both(j, _):
             straight(nz // 2 - 1 - j)
@@ -382,10 +317,10 @@
     for h in range(PIECES):
         arrived("sent", s5.at[h], db_send.at[h], na * nz - 1)
 
-    for k in range(chunks):
-        arrived("sent", s1.at[k], a_send.at[k], na - 1)
-        if k < obs_chunks:
-            arrived("sent", s2.at[k], z_send.at[k], nz - 1)
+    for part, sem in (
+        (s1.at[:, pl.ds(0, na - 1)], a_send), (s2.at[:, pl.ds(0, nz - 1)], z_send)
+    ):
+        pltpu.make_async_copy(part, part, sem).wait()
     for half in range(PIECES):
         arrived("sent", s2p.at[half], p_send.at[half], nz - 1)
 
@@ -428,13 +363,13 @@
                 pltpu.VMEM((PIECES, na * nz, OWN, HALF), bf16),
                 pltpu.VMEM((members, members), f32),
                 pltpu.VMEM((members, 1), f32),
-                dma((chunks, OWN)),
+                dma((chunks,)),
                 dma((2,)),
                 pltpu.SemaphoreType.REGULAR,
-                dma((chunks,)), dma((chunks,)),
-                dma((chunks - 1,)), dma((chunks - 1,)),
-                dma((2,)), dma((2,)),
-                dma((2,)), dma((2,)),
+                dma, dma((chunks,)),
+                dma, dma((chunks - 1,)),
+                dma((PIECES,)), dma((PIECES,)),
+                dma((PIECES,)), dma((PIECES,)),
             ],
             compiler_params=pltpu.CompilerParams(
                 collective_id=0, has_side_effects=True, vmem_limit_bytes=48 << 20

time: 55.5 us -> 55.1 us (level)
  no operation moved by 1% of the time
where the time goes in v7:
time: 55.1 us; the launch traced here: 54.9 us
  Pallas kernels  53.6 us (97%)
  local copies, waits for them, and re-layouts  0.66 us (1%)
  between operations  0.66 us (1%)
    pallas_call x1, Pallas kernels, local(): pl.pallas_call(functools.partial(kernel, nx, nz, nc), out_shape=jax.Shape...  53.6 us

profile of v7, /device:TPU:1, one launch (start us, length us, event | category | flops | bytes accessed | tf_op | source)
XLA Modules:
  0.0 54.9 jit_solution(3938061025156163184)
XLA Ops:
  0.7 53.6 %shard_map.55 = bf16[2,128,256]{2,1,0:T(8,128)(2,1)S(1)} custom-call(bf16[2,128,256]{2,1,0:T(8,128)(2,1)} %prior_hbm.1, bf16[2,128,1024]{2,1,0:T(8,128)(2,1)} %mapped_hbm.1, f32[1,1024]{1,0:T(1,128)} %dep_hbm.1, f32[1,1024]{1,0:T(1,128)} %prec_hbm.1, s32[1]{0:T(128)S(6)} %copy.7.lines_ref), custom_call_target="tpu_custom_call" | custom-call | tf_op jit(solution)/shard_map/pallas_call | solution.py:340
  54.3 0.7 %copy.8 = bf16[2,128,256]{2,1,0:T(8,128)(2,1)} copy(bf16[2,128,256]{2,1,0:T(8,128)(2,1)S(1)} %shard_map.55) | data formatting | bytes 262144

commit v8 on v7

--- a/solution.py
+++ b/solution.py
@@ -151,7 +151,7 @@
             z_copy(*copy_args, j - most).start()
             return 0
 
-        lax.fori_loop(0, most - least + 1, body, 0)
+        lax.fori_loop(0, most - least + 1, body, 0, unroll=True)
 
     def ring_far(*copy_args):
         z_copy(*copy_args, nz // 2).start()
@@ -307,7 +307,7 @@
             return 0
 
         straight(nz // 2)
-        lax.fori_loop(0, nz // 2 - 1, straight_both, 0)
+        lax.fori_loop(0, nz // 2 - 1, straight_both, 0, unroll=True)
         straight(0)
         db[h, z * na + a] = s5[h, z * na + a]
     for h in range(PIECES):

time: 55.1 us -> 55.1 us (level)
  no operation moved by 1% of the time
where the time goes in v8:
time: 55.1 us; the launch traced here: 54.9 us
  Pallas kernels  53.6 us (97%)
  local copies, waits for them, and re-layouts  0.66 us (1%)
  between operations  0.66 us (1%)
    pallas_call x1, Pallas kernels, local(): pl.pallas_call(functools.partial(kernel, nx, nz, nc), out_shape=jax.Shape...  53.6 us

profile of v8, /device:TPU:1, one launch (start us, length us, event | category | flops | bytes accessed | tf_op | source)
XLA Modules:
  0.0 54.9 jit_solution(12984128588431050401)
XLA Ops:
  0.7 53.6 %shard_map.55 = bf16[2,128,256]{2,1,0:T(8,128)(2,1)S(1)} custom-call(bf16[2,128,256]{2,1,0:T(8,128)(2,1)} %prior_hbm.1, bf16[2,128,1024]{2,1,0:T(8,128)(2,1)} %mapped_hbm.1, f32[1,1024]{1,0:T(1,128)} %dep_hbm.1, f32[1,1024]{1,0:T(1,128)} %prec_hbm.1, s32[1]{0:T(128)S(6)} %copy.7.lines_ref), custom_call_target="tpu_custom_call" | custom-call | tf_op jit(solution)/shard_map/pallas_call | solution.py:340
  54.3 0.7 %copy.8 = bf16[2,128,256]{2,1,0:T(8,128)(2,1)} copy(bf16[2,128,256]{2,1,0:T(8,128)(2,1)S(1)} %shard_map.55) | data formatting | bytes 262144

commit v9 on v8

--- a/solution.py
+++ b/solution.py
@@ -95,12 +95,12 @@
         pltpu.make_async_copy(dep_hbm, dep_ref, row_sem.at[0]),
         pltpu.make_async_copy(prec_hbm, prec_ref, row_sem.at[1]),
     ]
-    for copy in raw_copies(0):
-        copy.start()
     for step in range(near, 0, -1):
         signal_z(barrier, step)
         signal_z(barrier, -step)
-    lax.fori_loop(1, na, greet_a, 0)
+    lax.fori_loop(1, na, greet_a, 0, unroll=True)
+    for copy in raw_copies(0):
+        copy.start()
     for k in range(1, chunks):
         for copy in raw_copies(k):
             copy.start()

time: 55.1 us -> 55.1 us (level)
  no operation moved by 1% of the time
where the time goes in v9:
time: 55.1 us; the launch traced here: 54.9 us
  Pallas kernels  53.6 us (97%)
  local copies, waits for them, and re-layouts  0.66 us (1%)
  between operations  0.66 us (1%)
    pallas_call x1, Pallas kernels, local(): pl.pallas_call(functools.partial(kernel, nx, nz, nc), out_shape=jax.Shape...  53.6 us

profile of v9, /device:TPU:1, one launch (start us, length us, event | category | flops | bytes accessed | tf_op | source)
XLA Modules:
  0.0 54.9 jit_solution(6392009975432923865)
XLA Ops:
  0.7 53.6 %shard_map.55 = bf16[2,128,256]{2,1,0:T(8,128)(2,1)S(1)} custom-call(bf16[2,128,256]{2,1,0:T(8,128)(2,1)} %prior_hbm.1, bf16[2,128,1024]{2,1,0:T(8,128)(2,1)} %mapped_hbm.1, f32[1,1024]{1,0:T(1,128)} %dep_hbm.1, f32[1,1024]{1,0:T(1,128)} %prec_hbm.1, s32[1]{0:T(128)S(6)} %copy.7.lines_ref), custom_call_target="tpu_custom_call" | custom-call | tf_op jit(solution)/shard_map/pallas_call | solution.py:340
  54.3 0.7 %copy.8 = bf16[2,128,256]{2,1,0:T(8,128)(2,1)} copy(bf16[2,128,256]{2,1,0:T(8,128)(2,1)S(1)} %shard_map.55) | data formatting | bytes 262144
